TPU v7x, 128 devices: a whole 4x4x4 slice. The times are simulated.
128 devices in a mesh: seq: 16 (over y, z_lo, core), tensor: 8 (over z_hi, x).
Axes of the slice: x: 4, y: 4, z: 4 (z_hi: 2, z_lo: 2; z = z_hi * 2 + z_lo), core: 2. Of those that a mesh axis runs over, the one named last changes fastest.
Arguments:
- tokens: bfloat16 [8192, 8192], P('seq', 'tensor'), may hold values from -6 to 6
- positions: int32 [8192], P('seq'), may hold values from 0 to 8191, each once
- norm_gain: float32 [8192], replicated, may hold values from 0.1 to 1.9
- w_query: bfloat16 [8192, 4096], P('seq', 'tensor'), may hold values from -0.0625 to 0.0625
- w_key: bfloat16 [8192, 1024], P('seq', 'tensor'), may hold values from -0.0625 to 0.0625
- w_value: bfloat16 [8192, 1024], P('seq', 'tensor'), may hold values from -0.0625 to 0.0625
- b_query: float32 [4096], P('tensor'), may hold values from -40 to 40
- b_key: float32 [1024], P('tensor'), may hold values from -40 to 40
- b_value: float32 [1024], P('tensor'), may hold values from -6 to 6
- w_out: bfloat16 [4096, 8192], P('tensor', 'seq'), may hold values from -0.09375 to 0.09375
Outputs:
- mixed: bfloat16 [8192, 8192], P('seq', 'tensor')
- context: bfloat16 [8192, 4096], P('seq', 'tensor')
Inputs may be any that keep to these rules, and one draw needn't show every extreme that they name: positions holds every position 0 to 8191 once.
All inputs are finite; a program needn't handle non-finite values.
Results may differ from a plain program's by a relative error of at most 0.025.
Values may be sent and summed in bfloat16 or wider, within the bound.
A program may use at most 128 MiB of HBM per device.

v0:
```python
import math

import jax
import jax.numpy as jnp
from jax import lax
from jax.sharding import PartitionSpec as P

HD = 128


NORM_EPS = 1e-06
ROPE_BASE = 1000000.0
NEG_FILL = -1e30


def sent_together(arrays, axis, dim, along):
    ends, at = ([], 0)
    for a in arrays[:-1]:
        at += a.shape[along]
        ends.append(at)
    both = jnp.concatenate(arrays, axis=along)
    return tuple(jnp.split(lax.all_gather(both, axis, axis=dim, tiled=True), ends, axis=along))


def rotate(values_in, positions):
    half_dim = HD // 2
    inv_freq = ROPE_BASE ** (-jnp.arange(half_dim, dtype=jnp.float32) * 2.0 / HD)
    angles = positions.astype(jnp.float32)[:, None] * inv_freq[None, :]
    cosine = jnp.cos(angles)[:, None, :]
    sines = jnp.sin(angles)[:, None, :]
    lower_half = values_in[..., :half_dim]
    upper_half = values_in[..., half_dim:]
    return jnp.concatenate(
        [lower_half * cosine - upper_half * sines, upper_half * cosine + lower_half * sines], -1
    )


def shards(tokens, positions, norm_gain, w_query, w_key, w_value, b_query, b_key, b_value, w_out):
    tok_rows = tokens.shape[0]
    features = lax.all_gather(tokens, "tensor", axis=1, tiled=True)
    inputs = features.astype(jnp.float32)
    inverse_rms = lax.rsqrt(jnp.mean(inputs * inputs, -1, keepdims=True) + NORM_EPS)
    normed = (inputs * inverse_rms * norm_gain[None, :]).astype(jnp.bfloat16)
    w_cat = jnp.concatenate((w_query, w_key, w_value), 1)
    b_cat = jnp.concatenate((b_query, b_key, b_value))
    projected = jnp.dot(
        normed, lax.all_gather(w_cat, "seq", axis=0, tiled=True), preferred_element_type=jnp.float32
    )
    projected = projected + b_cat[None, :]
    query_cols = w_query.shape[1]
    key_cols = w_key.shape[1]
    heads_here = query_cols // HD
    kv_here = key_cols // HD
    group = heads_here // kv_here
    queries = rotate(projected[:, :query_cols].reshape(tok_rows, heads_here, HD), positions).astype(
        jnp.bfloat16
    )
    queries = queries.reshape(tok_rows, kv_here, group, HD)
    keys_rot = rotate(
        projected[:, query_cols : query_cols + key_cols].reshape(tok_rows, kv_here, HD), positions
    ).astype(jnp.bfloat16)
    values = (
        projected[:, query_cols + key_cols :].astype(jnp.bfloat16).reshape(tok_rows, kv_here, HD)
    )
    scale = HD ** (-0.5)

    def attend_block(running, key_block):
        running_max, denominator, numerator = running
        block_keys, block_values, key_pos = key_block
        scores = (
            jnp.einsum("tgcd,sgd->gcts", queries, block_keys, preferred_element_type=jnp.float32)
            * scale
        )
        allowed = (key_pos[None, :] <= positions[:, None])[None, None, :, :]
        scores = jnp.where(allowed, scores, NEG_FILL)
        new_max = jnp.maximum(running_max, jnp.max(scores, -1))
        weights = jnp.where(allowed, jnp.exp(scores - new_max[..., None]), 0.0)
        rescale = jnp.exp(running_max - new_max)
        denominator = denominator * rescale + jnp.sum(weights, -1)
        numerator = numerator * rescale[..., None] + jnp.einsum(
            "gcts,sgd->gctd",
            weights.astype(jnp.bfloat16),
            block_values,
            preferred_element_type=jnp.float32,
        )
        return (new_max, denominator, numerator)

    start_state = (
        jnp.full((kv_here, group, tok_rows), NEG_FILL, jnp.float32),
        jnp.zeros((kv_here, group, tok_rows), jnp.float32),
        jnp.zeros((kv_here, group, tok_rows, HD), jnp.float32),
    )
    all_keys_in, all_values_in, key_pos = (
        *sent_together((keys_rot, values), "seq", 0, 1),
        lax.all_gather(positions, "seq", axis=0, tiled=True),
    )
    count = all_keys_in.shape[0]
    width = math.gcd(count, 2048)
    stacked = (
        all_keys_in.reshape(count // width, width, kv_here, HD),
        all_values_in.reshape(count // width, width, kv_here, HD),
        key_pos.reshape(count // width, width),
    )

    def stepper(carried, key_block):
        return (attend_block(carried, key_block), None)

    result, unused = lax.scan(stepper, start_state, stacked)
    unused_max, denominator, numerator = result
    per_head = numerator / denominator[..., None]
    context = (
        jnp.transpose(per_head, (2, 0, 1, 3))
        .reshape(tok_rows, heads_here * HD)
        .astype(jnp.bfloat16)
    )
    out_terms = jnp.dot(
        context,
        lax.all_gather(w_out, "seq", axis=1, tiled=True),
        preferred_element_type=jnp.float32,
    )
    summed = lax.psum_scatter(
        out_terms.astype(jnp.bfloat16), "tensor", scatter_dimension=1, tiled=True
    ).astype(jnp.float32)
    mixed = (tokens.astype(jnp.float32) + summed).astype(jnp.bfloat16)
    return (mixed, context)


def solution(mesh):
    in_specs = (
        P("seq", "tensor"),
        P("seq"),
        P(),
        P("seq", "tensor"),
        P("seq", "tensor"),
        P("seq", "tensor"),
        P("tensor"),
        P("tensor"),
        P("tensor"),
        P("tensor", "seq"),
    )
    out_specs = (P("seq", "tensor"), P("seq", "tensor"))
    return jax.shard_map(shards, mesh=mesh, in_specs=in_specs, out_specs=out_specs, check_vma=False)
```

profile of v0, /device:TPU:0, one launch (start us, length us, event | category | flops | bytes accessed | tf_op | source)
XLA Modules:
  0.0 495.2 jit_solution(8700985036103313961)
XLA Ops:
  7.2 0.7 all-gather.6.cloned.1.call-update
  8.0 2.1 pad_maximum_fusion
  10.2 0.7 convert_element_type.55
  10.9 0.7 pad_maximum_fusion.3
  11.6 109.7 %all-gather.6.cloned.1.call-done = bf16[512,8192]{1,0:T(8,128)(2,1)} async-done(((bf16[512,1024]{1,0:T(8,128)(2,1)}), bf16[512,8192]{1,0:T(8,128)(2,1)}) %all-gather.6.cloned.1.call-update) | async-done | bytes 8388624 | tf_op jit(solution)/shard_map/all_gather | solution.py:40
  121.2 5.1 %fusion.25 = f32[512]{0:T(512)S(1)} fusion(bf16[512,8192]{1,0:T(8,128)(2,1)} %all-gather.6.cloned.1.call-done), kind=kLoop, calls=%fused_computation.31 | loop fusion | flops 12582400 | bytes 8390656 | tf_op jit(solution)/shard_map/reduce_sum | solution.py:42
  126.4 66.7 %all-gather.8.cloned.1.call-done = bf16[8192,768]{1,0:T(8,128)(2,1)} async-done(((bf16[512,768]{1,0:T(8,128)(2,1)}), bf16[8192,768]{1,0:T(8,128)(2,1)}) %all-gather.8.cloned.1.call-update) | async-done | bytes 12582928 | tf_op jit(solution)/shard_map/all_gather | solution.py:47
  193.1 12.5 %fusion.32 = f32[512,768]{0,1:T(8,128)S(1)} fusion(bf16[8192,768]{1,0:T(8,128)(2,1)} %all-gather.8.cloned.1.call-done, bf16[512,8192]{1,0:T(8,128)(2,1)} %all-gather.6.cloned.1.call-done, f32[8192]{0:T(1024)S(1)} %copy-done.5, f32[512]{0:T(512)S(1)} %add_rsqrt_fusion, f32[768]{0:T(1024)S(1)} %pad_maximum_fusion.3), kind=kOutput, calls=%fused_computation.39 | convolution fusion | flops 6459621376 | bytes 22582272 | tf_op jit(solution)/shard_map/dot_general | solution.py:46
  205.7 0.6 fusion.43
  206.2 0.7 pad_maximum_fusion.2
  207.0 0.5 all-gather.12.cloned.1.call-update
  207.6 1.0 multiply_cosine_fusion
  208.6 19.0 %all-gather = s32[16,1,512]{2,1,0:T(1,128)S(1)} all-gather(s32[1,1,512]{2,1,0:T(1,128)S(1)} %bitcast.114), channel_id=1, replica_groups=mesh['seq'=16,'tensor'=8] {'seq'}, dimensions={0}, use_global_device_ids=true | all-gather | bytes 34816 | tf_op jit(solution)/shard_map/all_gather | solution.py:95
  227.8 0.1 fusion.48
  227.9 0.3 copy.35
  228.3 0.3 copy.36
  228.6 0.3 fusion.35
  228.9 1.1 pad_maximum_fusion.1
  230.0 15.2 %all-gather.10.cloned.1.call-done = bf16[8192,2,128]{0,2,1:T(8,128)(2,1)} async-done(((bf16[512,2,128]{0,2,1:T(8,128)(2,1)}), bf16[8192,2,128]{0,2,1:T(8,128)(2,1)}) %all-gather.10.cloned.1.call-update) | async-done | bytes 4194320 | tf_op jit(solution)/shard_map/all_gather | solution.py:22
  245.2 3.9 fusion.47
  249.2 4.1 copy.33
  253.2 2.4 copy.34
  255.7 103.9 %while.15 = (s32[]{:T(128)}, f32[1,4,512]{2,1,0:T(4,128)S(1)}, f32[1,4,512]{2,1,0:T(4,128)S(1)}, f32[1,4,512,128]{3,2,1,0:T(8,128)S(1)}, s32[4,2048]{1,0:T(4,128...) while((s32[]{:T(128)}, f32[1,4,512]{2,1,0:T(4,128)S(1)}, ...), condition=%wide.region_4.5_spmd.clone, body=%wide.region_1.4_spmd.clone.sunk | while | flops 2203856896 | bytes 125463704 | solution.py:108
  255.7 0.8 broadcast_compare_fusion.2
  256.5 10.1 %fusion.60 = (f32[4,512]{1,0:T(4,128)S(1)}, f32[2048,512,4]{1,0,2:T(8,128)}) fusion(pred[512,2048]{0,1:T(8,128)(4,1)S(1)} %broadcast_compare_fusion.2, bf16[512,1,4,128]{3,0,2,1:T(8,128)(2,1)} %get-tuple-element.233, bf16[4,2048,1,128]{3,1,2,0:T(8,128)(2,1)} %get-tuple-element.232, s32[]{:T(128)} %get-tuple-element.215), kind=kOutput, calls=%fused_computation.2.clone.1 | convolution fusion | flops 1086322688 | bytes 18883072 | tf_op jit(solution)/shard_map/while/body/eval_jaxpr/tgcd,sgd->gcts/dot_general | solution.py:71
  266.6 9.0 %fusion.63 = f32[1,4,512,128]{3,2,1,0:T(8,128)S(1)} fusion(f32[2048,512,4]{1,0,2:T(8,128)} %get-tuple-element.202, f32[4,512]{1,0:T(4,128)S(1)} %bitcast.105, pred[512,2048]{0,1:T(8,128)(4,1)S(1)} %broadcast_compare_fusion.2, f32[1,4,512,128]{3,2,1,0:T(8,128)S(1)} %get-tuple-element.218, bf16[4,2048,1,128]{3,1,2,0:T(8,128)(2,1)} %get-tuple-element.234, ...), kind=kOutput, calls=%fused_computation.10.clone.1 | convolution fusion | flops 1095499776 | bytes 20464128 | tf_op jit(solution)/shard_map/while/body/eval_jaxpr/gcts,sgd->gctd/dot_general | solution.py:80
  275.6 2.3 copy-done
  277.9 4.2 fusion.62
  282.2 0.8 broadcast_compare_fusion.2
  282.9 10.2 %fusion.60 = (f32[4,512]{1,0:T(4,128)S(1)}, f32[2048,512,4]{1,0,2:T(8,128)}) fusion(pred[512,2048]{0,1:T(8,128)(4,1)S(1)} %broadcast_compare_fusion.2, bf16[512,1,4,128]{3,0,2,1:T(8,128)(2,1)} %get-tuple-element.233, bf16[4,2048,1,128]{3,1,2,0:T(8,128)(2,1)} %get-tuple-element.232, s32[]{:T(128)} %get-tuple-element.215), kind=kOutput, calls=%fused_computation.2.clone.1 | convolution fusion | flops 1086322688 | bytes 18883072 | tf_op jit(solution)/shard_map/while/body/eval_jaxpr/tgcd,sgd->gcts/dot_general | solution.py:71
  293.1 8.8 %fusion.63 = f32[1,4,512,128]{3,2,1,0:T(8,128)S(1)} fusion(f32[2048,512,4]{1,0,2:T(8,128)} %get-tuple-element.202, f32[4,512]{1,0:T(4,128)S(1)} %bitcast.105, pred[512,2048]{0,1:T(8,128)(4,1)S(1)} %broadcast_compare_fusion.2, f32[1,4,512,128]{3,2,1,0:T(8,128)S(1)} %get-tuple-element.218, bf16[4,2048,1,128]{3,1,2,0:T(8,128)(2,1)} %get-tuple-element.234, ...), kind=kOutput, calls=%fused_computation.10.clone.1 | convolution fusion | flops 1095499776 | bytes 20464128 | tf_op jit(solution)/shard_map/while/body/eval_jaxpr/gcts,sgd->gctd/dot_general | solution.py:80
  302.0 2.0 copy-done
  304.0 4.2 fusion.62
  308.2 0.8 broadcast_compare_fusion.2
  309.0 10.0 %fusion.60 = (f32[4,512]{1,0:T(4,128)S(1)}, f32[2048,512,4]{1,0,2:T(8,128)}) fusion(pred[512,2048]{0,1:T(8,128)(4,1)S(1)} %broadcast_compare_fusion.2, bf16[512,1,4,128]{3,0,2,1:T(8,128)(2,1)} %get-tuple-element.233, bf16[4,2048,1,128]{3,1,2,0:T(8,128)(2,1)} %get-tuple-element.232, s32[]{:T(128)} %get-tuple-element.215), kind=kOutput, calls=%fused_computation.2.clone.1 | convolution fusion | flops 1086322688 | bytes 18883072 | tf_op jit(solution)/shard_map/while/body/eval_jaxpr/tgcd,sgd->gcts/dot_general | solution.py:71
  319.0 8.7 %fusion.63 = f32[1,4,512,128]{3,2,1,0:T(8,128)S(1)} fusion(f32[2048,512,4]{1,0,2:T(8,128)} %get-tuple-element.202, f32[4,512]{1,0:T(4,128)S(1)} %bitcast.105, pred[512,2048]{0,1:T(8,128)(4,1)S(1)} %broadcast_compare_fusion.2, f32[1,4,512,128]{3,2,1,0:T(8,128)S(1)} %get-tuple-element.218, bf16[4,2048,1,128]{3,1,2,0:T(8,128)(2,1)} %get-tuple-element.234, ...), kind=kOutput, calls=%fused_computation.10.clone.1 | convolution fusion | flops 1095499776 | bytes 20464128 | tf_op jit(solution)/shard_map/while/body/eval_jaxpr/gcts,sgd->gctd/dot_general | solution.py:80
  327.7 2.0 copy-done
  329.7 4.2 fusion.62
  333.9 0.8 broadcast_compare_fusion.2
  334.7 10.0 %fusion.60 = (f32[4,512]{1,0:T(4,128)S(1)}, f32[2048,512,4]{1,0,2:T(8,128)}) fusion(pred[512,2048]{0,1:T(8,128)(4,1)S(1)} %broadcast_compare_fusion.2, bf16[512,1,4,128]{3,0,2,1:T(8,128)(2,1)} %get-tuple-element.233, bf16[4,2048,1,128]{3,1,2,0:T(8,128)(2,1)} %get-tuple-element.232, s32[]{:T(128)} %get-tuple-element.215), kind=kOutput, calls=%fused_computation.2.clone.1 | convolution fusion | flops 1086322688 | bytes 18883072 | tf_op jit(solution)/shard_map/while/body/eval_jaxpr/tgcd,sgd->gcts/dot_general | solution.py:71
  344.7 8.7 %fusion.63 = f32[1,4,512,128]{3,2,1,0:T(8,128)S(1)} fusion(f32[2048,512,4]{1,0,2:T(8,128)} %get-tuple-element.202, f32[4,512]{1,0:T(4,128)S(1)} %bitcast.105, pred[512,2048]{0,1:T(8,128)(4,1)S(1)} %broadcast_compare_fusion.2, f32[1,4,512,128]{3,2,1,0:T(8,128)S(1)} %get-tuple-element.218, bf16[4,2048,1,128]{3,1,2,0:T(8,128)(2,1)} %get-tuple-element.234, ...), kind=kOutput, calls=%fused_computation.10.clone.1 | convolution fusion | flops 1095499776 | bytes 20464128 | tf_op jit(solution)/shard_map/while/body/eval_jaxpr/gcts,sgd->gctd/dot_general | solution.py:80
  353.4 2.0 copy-done
  355.4 4.2 fusion.62
  359.6 0.3 fusion.37
  360.0 0.4 copy.30
  360.5 10.2 %convolution_convert_fusion = bf16[512,8192]{1,0:T(8,128)(2,1)} fusion(bf16[512,512]{1,0:T(8,128)(2,1)S(1)} %bitcast.111, bf16[512,8192]{1,0:T(8,128)(2,1)} %all-gather.12.cloned.1.call-done), kind=kOutput, calls=%fused_computation.34 | convolution fusion | flops 4299161600 | bytes 17301504 | tf_op jit(solution)/shard_map/dot_general | solution.py:116
  370.8 115.3 %reduce-scatter.2.cloned.1.call-done = bf16[512,1024]{1,0:T(8,128)(2,1)} async-done(((bf16[512,8192]{1,0:T(8,128)(2,1)}), bf16[512,1024]{1,0:T(8,128)(2,1)}) %reduce-scatter.2.cloned.1.call-update) | async-done | bytes 1048592 | tf_op jit(solution)/shard_map/reduce_scatter | solution.py:121
  486.0 2.6 add_convert_fusion
  (50 shorter events, 0.8 us)
Async XLA Ops:
  7.2 185.9 %copy-start.5 = (f32[8192]{0:T(1024)S(1)}, f32[8192]{0:T(1024)}, u32[]{:S(2)}) copy-start(f32[8192]{0:T(1024)} %param.14) | copy-start | bytes 98308
  7.2 114.1 %all-gather.6.cloned.1.call-start = ((), (), s32[]{:S(2)}) async-start(), calls=%async_computation.1 | async-start | bytes 9437184 | tf_op jit(solution)/shard_map/all_gather | solution.py:40
  7.9 185.2 %all-gather.8.cloned.1.call-start = ((), (), s32[]{:S(2)}) async-start(), calls=%async_computation.2 | async-start | bytes 13369344 | tf_op jit(solution)/shard_map/all_gather | solution.py:47
  10.1 235.1 %all-gather.10.cloned.1.call-start = ((), (), s32[]{:S(2)}) async-start(), calls=%async_computation.3 | async-start | bytes 4456448 | tf_op jit(solution)/shard_map/all_gather | solution.py:22
  126.3 82.3 %copy-start.4 = (s32[512]{0:T(512)S(1)}, s32[512]{0:T(512)}, u32[]{:S(2)}) copy-start(s32[512]{0:T(512)} %param.13) | copy-start | bytes 6148
  207.0 153.5 %all-gather.12.cloned.1.call-start = ((), (), s32[]{:S(2)}) async-start(), calls=%async_computation.4 | async-start | bytes 8912896 | tf_op jit(solution)/shard_map/all_gather | solution.py:118
  207.6 278.5 %reduce-scatter.2.cloned.1.call-start = ((), (), s32[]{:S(2)}) async-start(), calls=%async_computation.5 | async-start | bytes 9437184 | tf_op jit(solution)/shard_map/reduce_scatter | solution.py:121
  230.0 25.7 %copy-start.2 = (f32[1,4,512,128]{3,2,1,0:T(8,128)S(1)}, f32[1,4,512,128]{3,2,1,0:T(8,128)}, u32[]{:S(2)}) copy-start(f32[1,4,512,128]{3,2,1,0:T(8,128)} %custom-call.2) | copy-start | bytes 3145732
  266.6 11.3 %copy-start = (f32[2048,512,4]{1,0,2:T(8,128)S(1)}, f32[2048,512,4]{1,0,2:T(8,128)}, u32[]{:S(2)}) copy-start(f32[2048,512,4]{1,0,2:T(8,128)} %get-tuple-element.202) | copy-start | bytes 50331652 | tf_op jit(solution)/shard_map/while
  293.1 10.9 %copy-start = (f32[2048,512,4]{1,0,2:T(8,128)S(1)}, f32[2048,512,4]{1,0,2:T(8,128)}, u32[]{:S(2)}) copy-start(f32[2048,512,4]{1,0,2:T(8,128)} %get-tuple-element.202) | copy-start | bytes 50331652 | tf_op jit(solution)/shard_map/while
  319.0 10.7 %copy-start = (f32[2048,512,4]{1,0,2:T(8,128)S(1)}, f32[2048,512,4]{1,0,2:T(8,128)}, u32[]{:S(2)}) copy-start(f32[2048,512,4]{1,0,2:T(8,128)} %get-tuple-element.202) | copy-start | bytes 50331652 | tf_op jit(solution)/shard_map/while
  344.7 10.7 %copy-start = (f32[2048,512,4]{1,0,2:T(8,128)S(1)}, f32[2048,512,4]{1,0,2:T(8,128)}, u32[]{:S(2)}) copy-start(f32[2048,512,4]{1,0,2:T(8,128)} %get-tuple-element.202) | copy-start | bytes 50331652 | tf_op jit(solution)/shard_map/while
  360.5 10.3 %copy-start.3 = (bf16[64,8,4,128]{3,1,2,0:T(8,128)(2,1)}, bf16[64,8,4,128]{3,1,2,0:T(8,128)(2,1)S(1)}, u32[]{:S(2)}) copy-start(bf16[64,8,4,128]{3,1,2,0:T(8,128)(2,1)S(1)} %copy.39) | copy-start | bytes 1572868
  370.7 115.3 %copy-start.1 = (bf16[512,1024]{1,0:T(8,128)(2,1)S(1)}, bf16[512,1024]{1,0:T(8,128)(2,1)}, u32[]{:S(2)}) copy-start(bf16[512,1024]{1,0:T(8,128)(2,1)} %param.12) | copy-start | bytes 3145732
Sparse Core Ops, SparseCore 0:
  10.3 110.8 all-gather.5
  123.5 69.5 all-gather.7
  207.1 38.0 all-gather.9
  246.8 52.1 all-gather.11
  370.9 115.1 reduce-scatter.1
where the time goes:
time: 496 us; the launch traced here: 495 us
  waiting for transfers between devices  308 us (62%)
  matrix products  98.3 us (20%)
  other arithmetic  35.1 us (7%)
  local copies, waits for them, and re-layouts  20.2 us (4%)
  blocking collectives  19 us (4%)
  between operations  14 us (3%)
    reduce_scatter x1, waiting for transfers between devices, shards(): lax.psum_scatter(out_terms.astype(jnp.bfloat16), 'tensor', scatter_dimens...  115 us
    all_gather x1, waiting for transfers between devices, shards(): features = lax.all_gather(tokens, 'tensor', axis=1, tiled=True)  110 us
    all_gather x1, waiting for transfers between devices, shards(): lax.all_gather(w_cat, 'seq', axis=0, tiled=True)  66.7 us
    dot_general x4, matrix products, attend_block(): jnp.einsum('tgcd,sgd->gcts', queries, block_keys, preferred_element_type=...  40.3 us
    dot_general x4, matrix products, attend_block(): jnp.einsum('gcts,sgd->gctd', weights.astype(jnp.bfloat16), block_values,...  35.2 us
    all_gather x1, blocking collectives, shards(): lax.all_gather(positions, 'seq', axis=0, tiled=True)  19 us
    reduce_sum x4, other arithmetic, attend_block(): denominator = denominator * rescale + jnp.sum(weights, -1)  16.6 us
    all_gather x1, waiting for transfers between devices, sent_together(): lax.all_gather(both, axis, axis=dim, tiled=True)  15.2 us
  transfers between devices with their start and end apart: 5, of which 4 were waited for; matrix products, arithmetic and copies ran while one was open for 24% of the time, Pallas kernels for 0%

commit v1 on v0

v1 whole, which is shorter than its diff:
```python
import functools
import math

import jax
import jax.numpy as jnp
from jax import lax
from jax.experimental import pallas as pl
from jax.experimental.pallas import tpu as pltpu
from jax.sharding import PartitionSpec as P

HD = 128
NORM_EPS = 1e-06
ROPE_BASE = 1000000.0
NEG_FILL = -1e30
MESH = pl.DeviceIdType.MESH
BF16 = jnp.bfloat16
F32 = jnp.float32


def coords():
    s, t = lax.axis_index("seq"), lax.axis_index("tensor")
    return dict(y=s // 4, zl=(s // 2) % 2, c=s % 2, zh=t // 4, x=t % 4)


SIZES = dict(y=4, zl=2, c=2, zh=2, x=4)


def moved(k, **shift):
    k = dict(k)
    for name, by in shift.items():
        k[name] = (k[name] + (by + SIZES[name])) % SIZES[name]
    return k


def seq_of(k):
    return k["y"] * 4 + k["zl"] * 2 + k["c"]


def tensor_of(k):
    return k["zh"] * 4 + k["x"]


def device(k):
    return (seq_of(k), tensor_of(k))


class Gather:
    def __init__(self, k, slot, half_rows, ring, pair, sibling, ssem, rsem, base=0):
        self.k, self.slot, self.half = k, slot, half_rows
        self.ring, self.pair, self.sibling = ring, pair, sibling
        self.ssem, self.rsem, self.base = ssem, rsem, base
        self.sent = []

    def at(self, r=0, p=0, c=0):
        return (r, p, c)

    def place(self, where):
        r, p, c = where
        return moved(self.k, **{self.ring: r, self.pair: p, "c": c})

    def copy(self, i, block, target, half):
        ref = self.slot(self.place(block))
        if half is not None:
            ref = ref.at[pl.ds(half * self.half, self.half)]
        return pltpu.make_async_remote_copy(
            src_ref=ref,
            dst_ref=ref,
            send_sem=self.ssem.at[self.base + i],
            recv_sem=self.rsem.at[self.base + i],
            device_id=device(self.place(target)),
            device_id_type=MESH,
        )

    def send(self, i, block, target, half=None):
        self.copy(i, block, target, half).start()
        self.sent.append((i, block, target, half))

    def recv(self, i, block, half=None):
        self.copy(i, block, (0, 0, 1) if self.sibling else (1, 0, 0), half).wait_recv()

    def share(self, i, block):
        if self.sibling:
            self.send(i, block, self.at(c=1))

    def s0(self):
        own = self.at()
        self.send(0, own, self.at(1))
        self.send(1, own, self.at(-1))
        self.send(2, own, self.at(p=1))
        self.share(3, own)

    def s1(self):
        self.recv(0, self.at(-1))
        self.send(4, self.at(-1), self.at(1), 0)
        self.share(5, self.at(-1))
        self.recv(1, self.at(1))
        self.send(6, self.at(1), self.at(-1), 1)
        self.share(7, self.at(1))

    def s2(self):
        self.recv(2, self.at(p=1))
        self.send(8, self.at(p=1), self.at(1))
        self.send(9, self.at(p=1), self.at(-1))
        self.share(10, self.at(p=1))

    def s3(self):
        self.recv(4, self.at(2), 0)
        self.recv(6, self.at(2), 1)
        self.share(11, self.at(2))
        if not self.sibling:
            self.send(13, self.at(2), self.at(p=1))

    def s4(self):
        self.recv(8, self.at(-1, 1))
        if self.sibling:
            self.send(13, self.at(-1, 1), self.at(1), 0)
        self.share(14, self.at(-1, 1))
        self.recv(9, self.at(1, 1))
        if self.sibling:
            self.send(15, self.at(1, 1), self.at(-1), 1)
        self.share(16, self.at(1, 1))

    def s5(self):
        if self.sibling:
            self.recv(13, self.at(2, 1), 0)
            self.recv(15, self.at(2, 1), 1)
            self.share(17, self.at(2, 1))
        else:
            self.recv(13, self.at(2, 1))

    SHARED = {(0, 0): 3, (-1, 0): 5, (1, 0): 7, (0, 1): 10, (2, 0): 11, (-1, 1): 14, (1, 1): 16, (2, 1): 17}

    def recv_sibling(self, r, p):
        self.recv(self.SHARED[(r, p)], self.at(r, p, 1))

    def finish(self):
        for i, block, target, half in self.sent:
            self.copy(i, block, target, half).wait_send()


ORDER = ((0, 0), (-1, 0), (1, 0), (0, 1), (2, 0), (-1, 1), (1, 1), (2, 1))


def pick(index, values):
    out = values[0]
    for i, v in enumerate(values[1:], 1):
        out = jnp.where(index == i, v, out)
    return out


def greet(k, peers):
    barrier = pltpu.get_barrier_semaphore()
    for p in peers:
        pl.semaphore_signal(barrier, inc=1, device_id=device(p), device_id_type=MESH)
    pl.semaphore_wait(barrier, len(peers))


def tensor_peers(k):
    return [moved(k, x=r, zh=p) for r, p in ORDER[1:]]


def seq_peers(k):
    return [
        moved(k, y=r, zl=p, c=c) for r, p in ORDER for c in (0, 1) if (r, p, c) != (0, 0, 0)
    ]


def as_columns(rows):
    parts = [jnp.broadcast_to(rows[i : i + 1, :], (128, 128)).T for i in range(rows.shape[0])]
    return jnp.concatenate(parts, 0)


def project_kernel(
    tokens, pos, gain, w_query, w_key, w_value, bias, cosine, sine, w_out,
    q_out, kv_out, pos_out, wo_out,
    x_all, w_all, acc, normed, ssq, inverse,
    local_sem, x_ssem, x_rsem, w_ssem, w_rsem, s_ssem, s_rsem, p_ssem, p_rsem, t_ssem, t_rsem,
):
    k = coords()
    me_s, me_t = seq_of(k), tensor_of(k)
    rows = tokens.shape[0]
    qc, kc = w_query.shape[1], w_key.shape[1]
    wrows = w_query.shape[0]

    loads = [
        pltpu.make_async_copy(tokens, x_all.at[me_t], local_sem.at[0]),
        pltpu.make_async_copy(w_query, w_all.at[me_s, :, pl.ds(0, qc)], local_sem.at[1]),
        pltpu.make_async_copy(w_key, w_all.at[me_s, :, pl.ds(qc, kc)], local_sem.at[2]),
        pltpu.make_async_copy(w_value, w_all.at[me_s, :, pl.ds(qc + kc, kc)], local_sem.at[3]),
    ]
    for c in loads:
        c.start()
    pos_out[me_s] = pos[...]

    pair_t, pair_s = me_s // 2, me_t * 2 + k["c"]
    stays = me_t == pair_t
    t_k = dict(y=pair_s // 4, zl=(pair_s // 2) % 2, c=k["c"], zh=pair_t // 4, x=pair_t % 4)
    barrier = pltpu.get_barrier_semaphore()
    peers = tensor_peers(k) + seq_peers(k)
    for p in peers:
        pl.semaphore_signal(barrier, inc=1, device_id=device(p), device_id_type=MESH)

    @pl.when(jnp.logical_not(stays))
    def _():
        pl.semaphore_signal(barrier, inc=1, device_id=(pair_s, pair_t), device_id_type=MESH)

    pl.semaphore_wait(barrier, len(peers) + jnp.where(stays, 0, 1))

    xg = Gather(k, lambda b: x_all.at[tensor_of(b)], rows // 2, "x", "zh", False, x_ssem, x_rsem)
    wg = Gather(k, lambda b: w_all.at[seq_of(b)], wrows // 2, "y", "zl", True, w_ssem, w_rsem)
    for c in loads:
        c.wait()
    xg.s0()
    wg.s0()

    for i in range(rows // 128):
        xb = x_all[me_t, pl.ds(i * 128, 128), :].astype(F32)
        total = jnp.sum(xb * xb, -1, keepdims=True)
        ssq[me_t, i : i + 1, :] = jnp.broadcast_to(total, (128, 128)).T[0:1, :]

    def pos_copy(i, b, target):
        ref = pos_out.at[seq_of(b)]
        return pltpu.make_async_remote_copy(
            ref, ref, p_ssem.at[i], p_rsem.at[i], device_id=device(target), device_id_type=MESH
        )

    s_list = [(r, p, c) for r, p in ORDER for c in (0, 1) if (r, p, c) != (0, 0, 0)]
    for i, (r, p, c) in enumerate(s_list):
        pos_copy(i, k, moved(k, y=r, zl=p, c=c)).start()

    def ssq_copy(i, b, target):
        ref = ssq.at[tensor_of(b)]
        return pltpu.make_async_remote_copy(
            ref, ref, s_ssem.at[i], s_rsem.at[i], device_id=device(target), device_id_type=MESH
        )

    for i, (r, p) in enumerate(ORDER[1:]):
        ssq_copy(i, k, moved(k, x=r, zh=p)).start()

    acc[...] = jnp.zeros_like(acc)

    xg.s1()
    wg.s1()
    wg.s2()

    def move_out():
        return pltpu.make_async_remote_copy(
            w_out, wo_out, t_ssem, t_rsem, device_id=(pair_s, pair_t), device_id_type=MESH
        )

    def keep_out():
        return pltpu.make_async_copy(w_out, wo_out, t_rsem)

    @pl.when(jnp.logical_not(stays))
    def _():
        move_out().start()

    @pl.when(stays)
    def _():
        keep_out().start()

    for i, (r, p) in enumerate(ORDER[1:]):
        ssq_copy(i, moved(k, x=-r, zh=p), k).wait_recv()
    total = ssq[0]
    for i in range(1, 8):
        total = total + ssq[i]
    scale = lax.rsqrt(total / (8 * x_all.shape[2]) + NORM_EPS)
    inverse[...] = as_columns(scale[0 : rows // 128, :])

    wg.s3()
    xg.s2()
    wg.s4()
    xg.s3()
    wg.s5()
    for r, p in ORDER:
        wg.recv_sibling(r, p)

    def block(step, carry):
        @pl.when(step == 5)
        def _():
            xg.recv(8, xg.at(-1, 1))

        @pl.when(step == 6)
        def _():
            xg.recv(9, xg.at(1, 1))

        @pl.when(step == 7)
        def _():
            xg.s5()

        dx = pick(step, [r % 4 for r, _ in ORDER])
        dz = pick(step, [p for _, p in ORDER])
        t = ((k["zh"] + dz) % 2) * 4 + (k["x"] + dx) % 4
        g = gain[t]
        for i in range(rows // 128):
            inv = inverse[pl.ds(i * 128, 128), :]
            for j in range(x_all.shape[2] // 128):
                piece = x_all[t, pl.ds(i * 128, 128), pl.ds(j * 128, 128)].astype(F32)
                normed[pl.ds(i * 128, 128), pl.ds(j * 128, 128)] = (
                    piece * inv * g[:, j * 128 : (j + 1) * 128]
                ).astype(BF16)
        part = jnp.dot(normed[:, 0:wrows], w_all[2 * t], preferred_element_type=F32)
        part = part + jnp.dot(
            normed[:, wrows : 2 * wrows], w_all[2 * t + 1], preferred_element_type=F32
        )
        acc[...] += part
        return carry

    lax.fori_loop(0, 8, block, 0)

    cos, sin = cosine[...], sine[...]
    heads = qc // HD
    for h in range(heads + 1):
        u = acc[:, h * HD : (h + 1) * HD] + bias[:, h * HD : (h + 1) * HD]
        turned = (u * cos + pltpu.roll(u, HD // 2, 1) * sin).astype(BF16)
        if h < heads:
            q_out[h] = turned
        else:
            kv_out[:, 0:HD] = turned
    kv_out[:, HD : 2 * HD] = (acc[:, qc + kc :] + bias[:, qc + kc :]).astype(BF16)

    for i, (r, p, c) in enumerate(s_list):
        pos_copy(i, moved(k, y=-r, zl=p, c=c), k).wait_recv()

    @pl.when(jnp.logical_not(stays))
    def _():
        move_out().wait()

    @pl.when(stays)
    def _():
        keep_out().wait()

    for i, (r, p, c) in enumerate(s_list):
        pos_copy(i, k, moved(k, y=r, zl=p, c=c)).wait_send()
    for i, (r, p) in enumerate(ORDER[1:]):
        ssq_copy(i, k, moved(k, x=r, zh=p)).wait_send()
    xg.finish()
    wg.finish()


QT = 128
CHUNKS = ((0, 2), (2, 1), (3, 1))


def attend_kernel(
    q, kv, pos_all, wo, tokens,
    mixed, context,
    kv_all, wo_all, ctx_all, tok, key_pos, own_pos, top, low, num, mixed_v,
    local_sem, kv_ssem, kv_rsem, wo_ssem, wo_rsem, c_ssem, c_rsem,
):
    k = coords()
    me_s, me_t = seq_of(k), tensor_of(k)
    heads, rows, _ = q.shape
    cw = heads * HD
    wo_load = pltpu.make_async_copy(wo, wo_all.at[pl.ds((me_s // 2) * cw, cw), pl.ds(k["c"] * cw, cw)], local_sem.at[1])
    loads = [
        pltpu.make_async_copy(kv, kv_all.at[pl.ds(me_s * rows, rows)], local_sem.at[0]),
        pltpu.make_async_copy(tokens, tok, local_sem.at[2]),
    ]
    for c in loads:
        c.start()
    wo_load.start()
    greet(k, tensor_peers(k) + seq_peers(k))
    loads[0].wait()

    kg = Gather(
        k, lambda b: kv_all.at[pl.ds(seq_of(b) * rows, rows)], rows // 2, "y", "zl", True, kv_ssem, kv_rsem
    )
    wg = Gather(
        k,
        lambda b: wo_all.at[pl.ds((seq_of(b) // 2) * cw, cw), pl.ds(b["c"] * cw, cw)],
        cw // 2, "y", "zl", True, wo_ssem, wo_rsem,
    )

    def ctx_slot(first, count):
        return lambda b: ctx_all.at[pl.ds(first * QT, count * QT), pl.ds(tensor_of(b) * cw, cw)]

    cg = [
        Gather(k, ctx_slot(f, n), n * QT // 2, "x", "zh", False, c_ssem, c_rsem, base=16 * i)
        for i, (f, n) in enumerate(CHUNKS)
    ]
    kg.s0()

    def spread(s, carry):
        for j in range(rows // 128):
            key_pos[s, :, j * 128 : (j + 1) * 128] = pos_all[s, j : j + 1, :]
        return carry

    lax.fori_loop(0, pos_all.shape[0], spread, 0)
    own_pos[...] = as_columns(pos_all[me_s][0 : rows // 128, :])
    top[...] = jnp.full_like(top, NEG_FILL)
    low[...] = jnp.zeros_like(low)
    num[...] = jnp.zeros_like(num)
    factor = HD ** (-0.5) / math.log(2.0)
    keys = 2 * rows

    events = {}

    def event(step, fn):
        events.setdefault(step, []).append(fn)

    event(0, lambda: kg.recv_sibling(0, 0))
    event(2, lambda: (kg.s1(), kg.s2(), kg.recv_sibling(-1, 0)))
    event(4, lambda: kg.recv_sibling(1, 0))
    event(6, lambda: (kg.recv_sibling(0, 1), kg.s3(), kg.s4(), wo_load.wait(), wg.s0()))
    event(8, lambda: kg.recv_sibling(2, 0))
    event(10, lambda: kg.recv_sibling(-1, 1))
    event(12, lambda: (kg.recv_sibling(1, 1), kg.s5()))
    event(14, lambda: kg.recv_sibling(2, 1))
    event(19, lambda: (wg.s1(), wg.s2()))
    event(28, lambda: (wg.s3(), wg.s4()))

    total_steps = 8 * (rows // QT)
    done_at = []
    at = 0
    for f, n in CHUNKS:
        at += 8 * n
        done_at.append(at)

    def close(i):
        f, n = CHUNKS[i]
        r = pl.ds(f * QT, n * QT)
        for h in range(heads):
            bottom = jnp.sum(low[h, r, :], -1, keepdims=True)
            ctx_all[r, pl.ds(pl.multiple_of(me_t * cw + h * HD, HD), HD)] = (num[h, r, :] / bottom).astype(BF16)

    def step(g, carry):
        for at, fns in sorted(events.items()):
            @pl.when(g == at)
            def _(fns=fns):
                for fn in fns:
                    fn()

        first = g < 16
        kb = jnp.where(first, g // 2, g % 8)
        tile = jnp.where(first, g % 2, g // 8)
        dy = pick(kb, [r % 4 for r, _ in ORDER])
        dz = pick(kb, [p for _, p in ORDER])
        block = ((k["y"] + dy) % 4) * 2 + (k["zl"] + dz) % 2
        kr = pl.ds(pl.multiple_of(block * keys, keys), keys)
        qr = pl.ds(pl.multiple_of(tile * QT, QT), QT)
        mine = own_pos[qr, :]

        def head(h, c):
            s = lax.dot_general(
                q[h, qr, :], kv_all[kr, 0:HD], (((1,), (1,)), ((), ())), preferred_element_type=F32
            )
            parts = []
            for j in range(keys // 128):
                kp = key_pos[block * 2 + j // (rows // 128), :, (j % (rows // 128)) * 128 : (j % (rows // 128) + 1) * 128]
                parts.append(jnp.where(kp <= mine, s[:, j * 128 : (j + 1) * 128], NEG_FILL))
            best = parts[0]
            for x in parts[1:]:
                best = jnp.maximum(best, x)
            old = top[h, qr, :]
            new = jnp.maximum(old, jnp.max(best, -1, keepdims=True))
            top[h, qr, :] = new
            alpha = jnp.exp2((old - new) * factor)
            weights, total = [], low[h, qr, :] * alpha
            for x in parts:
                w = jnp.exp2((x - new) * factor)
                total = total + w
                weights.append(w.astype(BF16))
            low[h, qr, :] = total
            num[h, qr, :] = num[h, qr, :] * alpha + jnp.dot(
                jnp.concatenate(weights, 1), kv_all[kr, HD : 2 * HD], preferred_element_type=F32
            )
            return c

        lax.fori_loop(0, heads, head, 0)
        return carry

    for i in range(len(CHUNKS) - 1):
        event(done_at[i], functools.partial(lambda i: (close(i), cg[i].s0()), i))
    event(26, lambda: (cg[0].s1(), cg[0].s2()))
    event(30, lambda: cg[0].s3())
    lax.fori_loop(0, total_steps, step, 0)

    last = len(CHUNKS) - 1
    close(last)
    cg[last].s0()
    put = pltpu.make_async_copy(ctx_all.at[:, pl.ds(pl.multiple_of(me_t * cw, cw), cw)], context, local_sem.at[3])
    put.start()
    for i in range(1, last + 1):
        cg[i].s1()
        cg[i].s2()
        if i == 1:
            wg.s5()
        cg[i].s3()
    for r, p in ORDER:
        wg.recv_sibling(r, p)
    loads[1].wait()

    def output(i):
        f, n = CHUNKS[i]
        for m in range(n):
            r = pl.ds((f + m) * QT, QT)

            def half(c, carry):
                cols = pl.ds(pl.multiple_of(c * 256, 256), 256)
                summed = jnp.dot(ctx_all[r, :], wo_all[:, cols], preferred_element_type=F32)
                mixed_v[r, cols] = (tok[r, cols].astype(F32) + summed).astype(BF16)
                return carry

            lax.fori_loop(0, tok.shape[1] // 256, half, 0)

    puts = []
    for i in range(last + 1):
        cg[i].s4()
        cg[i].s5()
        output(i)
        f, n = CHUNKS[i]
        r = pl.ds(f * QT, n * QT)
        c = pltpu.make_async_copy(mixed_v.at[r], mixed.at[r], local_sem.at[4 + i])
        c.start()
        puts.append(c)
    put.wait()
    for c in puts:
        c.wait()
    kg.finish()
    wg.finish()
    for x in cg:
        x.finish()


def shards(tokens, positions, norm_gain, w_query, w_key, w_value, b_query, b_key, b_value, w_out):
    rows, feats = tokens.shape
    qc, kc = w_query.shape[1], w_key.shape[1]
    wrows = w_query.shape[0]
    heads = qc // HD
    nt, ns = lax.axis_size("tensor"), lax.axis_size("seq")
    half = HD // 2
    inv_freq = ROPE_BASE ** (-jnp.arange(half, dtype=F32) * 2.0 / HD)
    angles = positions.astype(F32)[:, None] * inv_freq[None, :]
    cos, sin = jnp.cos(angles), jnp.sin(angles)
    cosine = jnp.concatenate([cos, cos], 1)
    sine = jnp.concatenate([-sin, sin], 1)
    bias = jnp.concatenate((b_query, b_key, b_value))[None, :]
    pos = jnp.pad(positions.astype(F32).reshape(rows // 128, 128), ((0, 8 - rows // 128), (0, 0)))
    any_, vmem = pl.BlockSpec(memory_space=pl.ANY), pl.BlockSpec(memory_space=pltpu.VMEM)
    dma = pltpu.SemaphoreType.DMA
    q, kv, pos_all, wo = pl.pallas_call(
        project_kernel,
        name="project",
        out_shape=(
            jax.ShapeDtypeStruct((heads, rows, HD), BF16),
            jax.ShapeDtypeStruct((rows, 2 * HD), BF16),
            jax.ShapeDtypeStruct((ns, 8, 128), F32),
            jax.ShapeDtypeStruct(w_out.shape, BF16),
        ),
        in_specs=[any_, vmem, vmem, any_, any_, any_, vmem, vmem, vmem, any_],
        out_specs=(vmem, vmem, vmem, any_),
        scratch_shapes=[
            pltpu.VMEM((nt, rows, feats), BF16),
            pltpu.VMEM((ns, wrows, qc + 2 * kc), BF16),
            pltpu.VMEM((rows, qc + 2 * kc), F32),
            pltpu.VMEM((rows, feats), BF16),
            pltpu.VMEM((nt, 8, 128), F32),
            pltpu.VMEM((rows, 128), F32),
            dma((4,)), dma((20,)), dma((20,)), dma((20,)), dma((20,)),
            dma((8,)), dma((8,)), dma((16,)), dma((16,)), dma, dma,
        ],
        compiler_params=pltpu.CompilerParams(
            collective_id=0, has_side_effects=True, vmem_limit_bytes=48 * 1024 * 1024
        ),
    )(tokens, pos, norm_gain.reshape(nt, 1, feats), w_query, w_key, w_value, bias, cosine, sine, w_out)
    mixed, context = pl.pallas_call(
        attend_kernel,
        name="attend",
        out_shape=(
            jax.ShapeDtypeStruct((rows, feats), BF16),
            jax.ShapeDtypeStruct((rows, qc), BF16),
        ),
        in_specs=[vmem, any_, vmem, any_, any_],
        out_specs=(any_, any_),
        scratch_shapes=[
            pltpu.VMEM((ns * rows, 2 * HD), BF16),
            pltpu.VMEM((nt * qc, feats), BF16),
            pltpu.VMEM((rows, nt * qc), BF16),
            pltpu.VMEM((rows, feats), BF16),
            pltpu.VMEM((ns, 1, rows), F32),
            pltpu.VMEM((rows, 128), F32),
            pltpu.VMEM((heads, rows, 128), F32),
            pltpu.VMEM((heads, rows, 128), F32),
            pltpu.VMEM((heads, rows, HD), F32),
            pltpu.VMEM((rows, feats), BF16),
            dma((8,)), dma((20,)), dma((20,)), dma((20,)), dma((20,)), dma((48,)), dma((48,)),
        ],
        compiler_params=pltpu.CompilerParams(
            collective_id=1, has_side_effects=True, vmem_limit_bytes=48 * 1024 * 1024
        ),
    )(q, kv, pos_all, wo, tokens)
    return (mixed, context)


def solution(mesh):
    in_specs = (
        P("seq", "tensor"),
        P("seq"),
        P(),
        P("seq", "tensor"),
        P("seq", "tensor"),
        P("seq", "tensor"),
        P("tensor"),
        P("tensor"),
        P("tensor"),
        P("tensor", "seq"),
    )
    out_specs = (P("seq", "tensor"), P("seq", "tensor"))
    return jax.shard_map(shards, mesh=mesh, in_specs=in_specs, out_specs=out_specs, check_vma=False)
```

time: 496 us -> 227 us (0.46)
  waiting for transfers between devices: 308 us -> 0 us
  Pallas kernels: 0 us -> 218 us
  matrix products: 98.3 us -> 0 us
  other arithmetic: 35.1 us -> 1.22 us
  blocking collectives: 19 us -> 0 us
  local copies, waits for them, and re-layouts: 20.2 us -> 5.9 us
  between operations: 14 us -> 0.74 us
    pallas_call x0 -> x2, Pallas kernels: none -> 218 us  [the longest x1 113 us: shards(): pl.pallas_call(project_kernel, name='project', out_shape=(jax.ShapeDtypeS...]
    all_gather x4 -> x0, waiting for transfers between devices: 192 us -> none  [the longest x1 110 us: shards(): features = lax.all_gather(tokens, 'tensor', axis=1, tiled=True)]
    reduce_scatter x1 -> x0, waiting for transfers between devices: 115 us -> none  [shards(): lax.psum_scatter(out_terms.astype(jnp.bfloat16), 'tensor', scatter_dimens...]
    dot_general x10 -> x0, matrix products: 98.3 us -> none  [the longest x4 40.3 us: attend_block(): jnp.einsum('tgcd,sgd->gcts', queries, block_keys, preferred_element_type=...]
    reduce_sum x5 -> x0, other arithmetic: 21.7 us -> none  [the longest x4 16.6 us: attend_block(): denominator = denominator * rescale + jnp.sum(weights, -1)]
    all_gather x1 -> x0, blocking collectives: 19 us -> none  [shards(): lax.all_gather(positions, 'seq', axis=0, tiled=True)]
    while x12 -> x0, local copies, waits for them, and re-layouts: 8.27 us -> none
  transfers between devices with their start and end apart: 5 -> 0, of which waited for: 4 -> 0; matrix products, arithmetic and copies ran while one was open for 24% -> 0% of each run, Pallas kernels for 0% -> 0%
where the time goes in v1:
time: 227 us; the launch traced here: 226 us
  Pallas kernels  218 us (96%)
  local copies, waits for them, and re-layouts  5.9 us (3%)
    pallas_call x1, Pallas kernels, shards(): pl.pallas_call(project_kernel, name='project', out_shape=(jax.ShapeDtypeS...  113 us
    pallas_call x1, Pallas kernels, shards(): pl.pallas_call(attend_kernel, name='attend', out_shape=(jax.ShapeDtypeStr...  105 us
    unnamed x22, local copies, waits for them, and re-layouts  5.89 us

profile of v1, /device:TPU:0, one launch (start us, length us, event | category | flops | bytes accessed | tf_op | source)
XLA Modules:
  0.0 226.0 jit_solution(4121326817354212176)
XLA Ops:
  0.6 0.0 copy-start.6
  0.6 0.0 copy-start.8
  0.7 0.0 copy-start.9
  0.7 0.6 copy-done.6
  1.3 0.0 copy-done.8
  1.3 0.0 copy-done.9
  1.3 0.0 copy-start.7
  1.3 0.0 copy-start.5
  1.4 0.6 copy-done.7
  2.0 0.0 copy-start
  2.0 1.0 fusion
  3.0 0.0 copy-start.1
  3.0 0.0 copy-start.2
  3.0 0.2 pad_maximum_fusion
  3.2 0.0 copy-done.5
  3.3 0.0 copy-done
  3.3 0.8 copy-done.1
  4.1 0.2 copy-done.2
  4.3 0.0 copy-start.3
  4.3 0.9 copy-done.3
  5.2 0.0 copy-start.4
  5.2 0.9 copy-done.4
  6.1 113.2 %project.1 = (bf16[4,512,128]{2,1,0:T(8,128)(2,1)S(1)}, bf16[512,256]{1,0:T(8,128)(2,1)S(1)}, f32[16,8,128]{2,1,0:T(8,128)S(1)}, bf16[512,512]{1,0:T(8,128)(2,1)S(1)}) custom-call(bf16[512,1024]{1,0:T(8,128)(2,1)S(1)} %copy-done, f32[8,128]{1,0:T(8,128)S(1)} %pad.4.pos, f32[8,1,1024]{2,1,0:T(1,128)S(1)} %bitcast.3, bf16[512,512]{1,0:T(8,128)(2,1)S(1)} %copy-done.1, ...), custom_call_target="tpu_custom_call" | custom-call | tf_op jit(solution)/shard_map/project/pallas_call | solution.py:542
  119.3 104.9 %attend.1 = (bf16[512,1024]{1,0:T(8,128)(2,1)S(1)}, bf16[512,512]{1,0:T(8,128)(2,1)S(1)}) custom-call(bf16[4,512,128]{2,1,0:T(8,128)(2,1)S(1)} %get-tuple-element.6.q, bf16[512,256]{1,0:T(8,128)(2,1)S(1)} %get-tuple-element.7.kv, f32[16,8,128]{2,1,0:T(8,128)S(1)} %get-tuple-element.8.pos_all, bf16[512,512]{1,0:T(8,128)(2,1)S(1)} %get-tuple-element.9.wo, ...), custom_call_target="tpu_custom_call" | custom-call | tf_op jit(solution)/shard_map/attend/pallas_call | solution.py:567
  224.2 1.0 copy.14
  225.2 0.8 copy.15
  (5 shorter events, 0.0 us)
Async XLA Ops:
  0.6 0.7 copy-start.6
  0.6 0.7 copy-start.8
  0.7 0.7 copy-start.9
  1.3 0.7 copy-start.7
  1.3 1.9 copy-start.5
  2.0 1.2 copy-start
  3.0 1.1 copy-start.1
  3.0 1.2 copy-start.2
  4.3 0.9 copy-start.3
  5.2 0.9 copy-start.4

commit v2 on v1

v2 whole, which is shorter than its diff:
```python
import functools
import math

import jax
import jax.numpy as jnp
from jax import lax
from jax.experimental import pallas as pl
from jax.experimental.pallas import tpu as pltpu
from jax.sharding import PartitionSpec as P

HD = 128
NORM_EPS = 1e-06
ROPE_BASE = 1000000.0
NEG_FILL = -1e30
MESH = pl.DeviceIdType.MESH
BF16 = jnp.bfloat16
F32 = jnp.float32


def coords():
    s, t = lax.axis_index("seq"), lax.axis_index("tensor")
    return dict(y=s // 4, zl=(s // 2) % 2, c=s % 2, zh=t // 4, x=t % 4)


SIZES = dict(y=4, zl=2, c=2, zh=2, x=4)


def moved(k, **shift):
    k = dict(k)
    for name, by in shift.items():
        k[name] = (k[name] + (by + SIZES[name])) % SIZES[name]
    return k


def seq_of(k):
    return k["y"] * 4 + k["zl"] * 2 + k["c"]


def tensor_of(k):
    return k["zh"] * 4 + k["x"]


def device(k):
    return (seq_of(k), tensor_of(k))


class Gather:
    def __init__(self, k, slot, half_rows, ring, pair, sibling, ssem, rsem, base=0):
        self.k, self.slot, self.half = k, slot, half_rows
        self.ring, self.pair, self.sibling = ring, pair, sibling
        self.ssem, self.rsem, self.base = ssem, rsem, base
        self.sent = []

    def at(self, r=0, p=0, c=0):
        return (r, p, c)

    def place(self, where):
        r, p, c = where
        return moved(self.k, **{self.ring: r, self.pair: p, "c": c})

    def copy(self, i, block, target, half):
        ref = self.slot(self.place(block))
        if half is not None:
            ref = ref.at[pl.ds(half * self.half, self.half)]
        return pltpu.make_async_remote_copy(
            src_ref=ref,
            dst_ref=ref,
            send_sem=self.ssem.at[self.base + i],
            recv_sem=self.rsem.at[self.base + i],
            device_id=device(self.place(target)),
            device_id_type=MESH,
        )

    def send(self, i, block, target, half=None):
        self.copy(i, block, target, half).start()
        self.sent.append((i, block, target, half))

    def recv(self, i, block, half=None):
        self.copy(i, block, (0, 0, 1) if self.sibling else (1, 0, 0), half).wait_recv()

    def share(self, i, block):
        if self.sibling:
            self.send(i, block, self.at(c=1))

    def s0(self):
        own = self.at()
        self.send(0, own, self.at(1))
        self.send(1, own, self.at(-1))
        if self.sibling:
            self.send(2, own, self.at(p=1))
        self.share(3, own)

    def pair_halves(self):
        self.send(2, self.at(), self.at(p=1), 0)
        self.send(3, self.at(), self.at(p=1), 1)

    def s1(self):
        self.recv(0, self.at(-1))
        self.send(4, self.at(-1), self.at(1), 0)
        self.share(5, self.at(-1))
        self.recv(1, self.at(1))
        self.send(6, self.at(1), self.at(-1), 1)
        self.share(7, self.at(1))

    def s2(self):
        self.recv(2, self.at(p=1))
        self.send(8, self.at(p=1), self.at(1))
        self.send(9, self.at(p=1), self.at(-1))
        self.share(10, self.at(p=1))

    def s2_half(self, h):
        self.recv(2 + h, self.at(p=1), h)
        self.send(8 + 2 * h, self.at(p=1), self.at(1), h)
        self.send(9 + 2 * h, self.at(p=1), self.at(-1), h)

    def s4_halves(self):
        for h in (0, 1):
            self.recv(8 + 2 * h, self.at(-1, 1), h)
            self.recv(9 + 2 * h, self.at(1, 1), h)

    def s3(self):
        self.recv(4, self.at(2), 0)
        self.recv(6, self.at(2), 1)
        self.share(11, self.at(2))
        if not self.sibling:
            self.send(13, self.at(2), self.at(p=1))

    def s4(self):
        self.recv(8, self.at(-1, 1))
        if self.sibling:
            self.send(13, self.at(-1, 1), self.at(1), 0)
        self.share(14, self.at(-1, 1))
        self.recv(9, self.at(1, 1))
        if self.sibling:
            self.send(15, self.at(1, 1), self.at(-1), 1)
        self.share(16, self.at(1, 1))

    def s5(self):
        if self.sibling:
            self.recv(13, self.at(2, 1), 0)
            self.recv(15, self.at(2, 1), 1)
            self.share(17, self.at(2, 1))
        else:
            self.recv(13, self.at(2, 1))

    SHARED = {(0, 0): 3, (-1, 0): 5, (1, 0): 7, (0, 1): 10, (2, 0): 11, (-1, 1): 14, (1, 1): 16, (2, 1): 17}

    def recv_sibling(self, r, p):
        self.recv(self.SHARED[(r, p)], self.at(r, p, 1))

    def finish(self):
        for i, block, target, half in self.sent:
            self.copy(i, block, target, half).wait_send()


ORDER = ((0, 0), (-1, 0), (1, 0), (0, 1), (2, 0), (-1, 1), (1, 1), (2, 1))


def pick(index, values):
    out = values[0]
    for i, v in enumerate(values[1:], 1):
        out = jnp.where(index == i, v, out)
    return out


def greet(k, peers):
    barrier = pltpu.get_barrier_semaphore()
    for p in peers:
        pl.semaphore_signal(barrier, inc=1, device_id=device(p), device_id_type=MESH)
    pl.semaphore_wait(barrier, len(peers))


def tensor_peers(k):
    return [moved(k, x=r, zh=p) for r, p in ORDER[1:]]


def seq_peers(k):
    return [
        moved(k, y=r, zl=p, c=c) for r, p in ORDER for c in (0, 1) if (r, p, c) != (0, 0, 0)
    ]


def as_columns(rows):
    parts = [jnp.broadcast_to(rows[i : i + 1, :], (128, 128)).T for i in range(rows.shape[0])]
    return jnp.concatenate(parts, 0)


QT = 128
CHUNKS = ((0, 2), (2, 1), (3, 1))
GROUP = 2


def block_kernel(
    tokens, pos, gain, w_query, w_key, w_value, bias, cosine, sine, w_out,
    mixed, context,
    x_all, w_all, acc, normed, ssq, inverse, wo_mid, pos_all,
    q, kv_all, wo_all, ctx_all, key_pos, own_pos, top, low, num, mixed_v,
    local_sem, x_ssem, x_rsem, w_ssem, w_rsem, s_ssem, s_rsem, p_ssem, p_rsem, t_ssem, t_rsem,
    kv_ssem, kv_rsem, wo_ssem, wo_rsem, c_ssem, c_rsem,
):
    k = coords()
    me_s, me_t = seq_of(k), tensor_of(k)
    rows = tokens.shape[0]
    qc, kc = w_query.shape[1], w_key.shape[1]
    wrows = w_query.shape[0]
    heads = qc // HD
    cw = qc

    loads = [
        pltpu.make_async_copy(tokens, x_all.at[me_t], local_sem.at[0]),
        pltpu.make_async_copy(w_query, w_all.at[me_s, :, pl.ds(0, qc)], local_sem.at[1]),
        pltpu.make_async_copy(w_key, w_all.at[me_s, :, pl.ds(qc, kc)], local_sem.at[2]),
        pltpu.make_async_copy(w_value, w_all.at[me_s, :, pl.ds(qc + kc, kc)], local_sem.at[3]),
        pltpu.make_async_copy(pos, pos_all.at[me_s], local_sem.at[4]),
    ]
    for c in loads:
        c.start()
    greet(k, tensor_peers(k) + seq_peers(k))
    for c in loads:
        c.wait()

    def wo_slot(b):
        return wo_all.at[:, seq_of(b) // 2, :, pl.ds(pl.multiple_of(b["c"] * cw, cw), cw)]

    def ctx_slot(first, count):
        return lambda b: ctx_all.at[
            pl.ds(first * QT, count * QT), pl.ds(pl.multiple_of(tensor_of(b) * cw, cw), cw)
        ]

    xg = Gather(k, lambda b: x_all.at[tensor_of(b)], rows // 2, "x", "zh", False, x_ssem, x_rsem)
    wg = Gather(k, lambda b: w_all.at[seq_of(b)], wrows // 2, "y", "zl", True, w_ssem, w_rsem)
    kg = Gather(
        k, lambda b: kv_all.at[pl.ds(pl.multiple_of(seq_of(b) * rows, rows), rows)], rows // 2,
        "y", "zl", True, kv_ssem, kv_rsem,
    )
    og = Gather(k, wo_slot, wo_all.shape[0] // 2, "y", "zl", True, wo_ssem, wo_rsem)
    cg = [
        Gather(k, ctx_slot(f, n), n * QT // 2, "x", "zh", False, c_ssem, c_rsem, base=16 * i)
        for i, (f, n) in enumerate(CHUNKS)
    ]

    eighth = wo_mid.shape[1]

    def spread_copy(i, source, target):
        return pltpu.make_async_remote_copy(
            w_out.at[pl.ds((seq_of(target) // 2) * eighth, eighth)], wo_mid.at[seq_of(source) // 2],
            t_ssem.at[i], t_rsem.at[i], device_id=device(target), device_id_type=MESH,
        )

    def wo_part(t):
        return wo_all.at[t, me_s // 2, :, pl.ds(pl.multiple_of(k["c"] * cw, cw), cw)]

    def settle_copy(i, source, target):
        return pltpu.make_async_remote_copy(
            wo_mid.at[tensor_of(target)], wo_part(tensor_of(source)),
            t_ssem.at[8 + i], t_rsem.at[8 + i], device_id=device(target), device_id_type=MESH,
        )

    spread_own = pltpu.make_async_copy(
        w_out.at[pl.ds((me_s // 2) * eighth, eighth)], wo_mid.at[me_s // 2], t_ssem.at[7]
    )
    settle_own = pltpu.make_async_copy(wo_mid.at[me_t], wo_part(me_t), t_ssem.at[15])

    def pos_copy(i, b, target):
        ref = pos_all.at[seq_of(b)]
        return pltpu.make_async_remote_copy(
            ref, ref, p_ssem.at[i], p_rsem.at[i], device_id=device(target), device_id_type=MESH
        )

    s_list = [(r, p, c) for r, p in ORDER for c in (0, 1) if (r, p, c) != (0, 0, 0)]

    def ssq_copy(i, b, target):
        ref = ssq.at[tensor_of(b)]
        return pltpu.make_async_remote_copy(
            ref, ref, s_ssem.at[i], s_rsem.at[i], device_id=device(target), device_id_type=MESH
        )

    wg.s0()
    xg.s0()
    for i in range(rows // 128):
        xb = x_all[me_t, pl.ds(i * 128, 128), :].astype(F32)
        total = jnp.sum(xb * xb, -1, keepdims=True)
        ssq[me_t, i : i + 1, :] = jnp.broadcast_to(total, (128, 128)).T[0:1, :]
    for i, (r, p) in enumerate(ORDER[1:]):
        spread_copy(i, k, moved(k, y=r, zl=p)).start()
    spread_own.start()
    for i, (r, p, c) in enumerate(s_list):
        pos_copy(i, k, moved(k, y=r, zl=p, c=c)).start()
    acc[...] = jnp.zeros_like(acc)
    top[...] = jnp.full_like(top, NEG_FILL)
    low[...] = jnp.zeros_like(low)
    num[...] = jnp.zeros_like(num)
    for i, (r, p) in enumerate(ORDER[1:]):
        ssq_copy(i, k, moved(k, x=r, zh=p)).start()

    wg.s1()
    wg.s2()
    xg.pair_halves()
    xg.s1()
    for i, (r, p) in enumerate(ORDER[1:]):
        ssq_copy(i, moved(k, x=-r, zh=p), k).wait_recv()
    total = ssq[0]
    for i in range(1, 8):
        total = total + ssq[i]
    scale = lax.rsqrt(total / (8 * x_all.shape[2]) + NORM_EPS)
    inverse[...] = as_columns(scale[0 : rows // 128, :])
    wg.s3()
    xg.s2_half(0)
    for i, (r, p) in enumerate(ORDER[1:]):
        spread_copy(i, moved(k, y=-r, zl=p), moved(k, y=r, zl=p)).wait_recv()
    spread_own.wait()
    for i, (r, p) in enumerate(ORDER[1:]):
        settle_copy(i, k, moved(k, x=r, zh=p)).start()
    settle_own.start()
    xg.s3()
    xg.s2_half(1)
    wg.s4()
    for i, (r, p, c) in enumerate(s_list):
        pos_copy(i, moved(k, y=-r, zl=p, c=c), k).wait_recv()

    def spread(s, carry):
        for j in range(rows // 128):
            key_pos[s, :, j * 128 : (j + 1) * 128] = pos_all[s, j : j + 1, :]
        return carry

    lax.fori_loop(0, pos_all.shape[0], spread, 0)
    own_pos[...] = as_columns(pos_all[me_s][0 : rows // 128, :])
    for i, (r, p) in enumerate(ORDER[1:]):
        settle_copy(i, moved(k, x=-r, zh=p), moved(k, x=r, zh=p)).wait_recv()
    settle_own.wait()
    og.s0()
    wg.s5()
    for r, p in ORDER:
        wg.recv_sibling(r, p)

    def block(step, carry):
        @pl.when(step == 5)
        def _():
            xg.s4_halves()

        @pl.when(step == 7)
        def _():
            xg.s5()

        dx = pick(step, [r % 4 for r, _ in ORDER])
        dz = pick(step, [p for _, p in ORDER])
        t = ((k["zh"] + dz) % 2) * 4 + (k["x"] + dx) % 4
        g = gain[t]
        for i in range(rows // 128):
            inv = inverse[pl.ds(i * 128, 128), :]
            for j in range(x_all.shape[2] // 128):
                piece = x_all[t, pl.ds(i * 128, 128), pl.ds(j * 128, 128)].astype(F32)
                normed[pl.ds(i * 128, 128), pl.ds(j * 128, 128)] = (
                    piece * inv * g[:, j * 128 : (j + 1) * 128]
                ).astype(BF16)
        part = jnp.dot(normed[:, 0:wrows], w_all[2 * t], preferred_element_type=F32)
        part = part + jnp.dot(
            normed[:, wrows : 2 * wrows], w_all[2 * t + 1], preferred_element_type=F32
        )
        acc[...] += part
        return carry

    lax.fori_loop(0, 8, block, 0)

    cos, sin = cosine[...], sine[...]
    mine_r = pl.ds(pl.multiple_of(me_s * rows, rows), rows)

    def turned(h):
        u = acc[:, h * HD : (h + 1) * HD] + bias[:, h * HD : (h + 1) * HD]
        return (u * cos + pltpu.roll(u, HD // 2, 1) * sin).astype(BF16)

    kv_all[mine_r, 0:HD] = turned(heads)
    kv_all[mine_r, HD : 2 * HD] = (acc[:, qc + kc :] + bias[:, qc + kc :]).astype(BF16)
    for h in range(heads):
        q[h] = turned(h)
    kg.s0()

    factor = HD ** (-0.5) / math.log(2.0)
    keys = 2 * rows
    tiles = rows // QT
    events = {}

    def event(step, *fns):
        events.setdefault(step, []).extend(fns)

    def sib(r, p):
        return lambda: kg.recv_sibling(r, p)

    def close(i):
        f, n = CHUNKS[i]
        r = pl.ds(f * QT, n * QT)
        for h in range(heads):
            bottom = jnp.sum(low[h, r, :], -1, keepdims=True)
            ctx_all[r, pl.ds(pl.multiple_of(me_t * cw + h * HD, HD), HD)] = (
                num[h, r, :] / bottom
            ).astype(BF16)

    def send_ctx(i):
        cg[i].s0()
        cg[i].pair_halves()

    event(0, sib(0, 0))
    event(4, kg.s1, sib(-1, 0))
    event(5, kg.s2)
    event(6, sib(1, 0))
    event(8, sib(0, 1))
    event(10, kg.s3, sib(2, 0))
    event(12, kg.s4, sib(-1, 1), og.s1)
    event(14, sib(1, 1))
    event(16, kg.s5, sib(2, 1), og.s2)
    event(18, lambda: close(0), lambda: send_ctx(0))
    event(24, cg[0].s1)
    event(25, lambda: close(1), lambda: send_ctx(1), lambda: cg[0].s2_half(0))
    event(27, lambda: cg[0].s2_half(1))
    event(29, cg[0].s3, og.s3)

    def step(g, carry):
        for at, fns in sorted(events.items()):
            @pl.when(g == at)
            def _(fns=fns):
                for fn in fns:
                    fn()

        late = jnp.maximum(g - 18, 0)
        mid = jnp.maximum(g - 4, 0)
        kb = jnp.where(g < 4, 0, jnp.where(g < 18, 1 + mid // 2, 1 + late % 7))
        tile = jnp.where(g < 4, g, jnp.where(g < 18, mid % 2, 2 + late // 7))
        dy = pick(kb, [r % 4 for r, _ in ORDER])
        dz = pick(kb, [p for _, p in ORDER])
        chip = ((k["y"] + dy) % 4) * 2 + (k["zl"] + dz) % 2
        kr = pl.ds(pl.multiple_of(chip * keys, keys), keys)
        qr = pl.ds(pl.multiple_of(tile * QT, QT), QT)
        mine = jnp.concatenate([own_pos[qr, :]] * GROUP, 0)
        gr = GROUP * QT

        def scores(u):
            hs = slice(u * GROUP, (u + 1) * GROUP)
            return lax.dot_general(
                q[hs, qr, :].reshape(gr, HD), kv_all[kr, 0:HD], (((1,), (1,)), ((), ())),
                preferred_element_type=F32,
            )

        def soften(u, s):
            hs = slice(u * GROUP, (u + 1) * GROUP)
            parts = []
            for j in range(keys // 128):
                at = (j % (rows // 128)) * 128
                kp = key_pos[chip * 2 + j // (rows // 128), :, at : at + 128]
                parts.append(jnp.where(kp <= mine, s[:, j * 128 : (j + 1) * 128], NEG_FILL))
            best = parts[0]
            for x in parts[1:]:
                best = jnp.maximum(best, x)
            old = top[hs, qr, :].reshape(gr, 128)
            new = jnp.maximum(old, jnp.max(best, -1, keepdims=True))
            top[hs, qr, :] = new.reshape(GROUP, QT, 128)
            alpha = jnp.exp2((old - new) * factor)
            weights, total = [], low[hs, qr, :].reshape(gr, 128) * alpha
            for x in parts:
                w = jnp.exp2((x - new) * factor)
                total = total + w
                weights.append(w.astype(BF16))
            low[hs, qr, :] = total.reshape(GROUP, QT, 128)
            return alpha, jnp.concatenate(weights, 1)

        def collect(u, alpha, weights):
            hs = slice(u * GROUP, (u + 1) * GROUP)
            out = num[hs, qr, :].reshape(gr, HD) * alpha + jnp.dot(
                weights, kv_all[kr, HD : 2 * HD], preferred_element_type=F32
            )
            num[hs, qr, :] = out.reshape(GROUP, QT, HD)

        units = heads // GROUP
        s, held = scores(0), None
        for u in range(units):
            later = scores(u + 1) if u + 1 < units else None
            now = soften(u, s)
            if held is not None:
                collect(u - 1, *held)
            s, held = later, now
        collect(units - 1, *held)
        return carry

    lax.fori_loop(0, 8 * tiles, step, 0)

    close(2)
    send_ctx(2)
    put = pltpu.make_async_copy(
        ctx_all.at[:, pl.ds(pl.multiple_of(me_t * cw, cw), cw)], context, local_sem.at[5]
    )
    put.start()
    cg[1].s1()
    cg[1].s2_half(0)
    cg[1].s2_half(1)
    og.s4()
    cg[1].s3()
    cg[2].s1()
    cg[2].s2_half(0)
    cg[2].s2_half(1)
    cg[2].s3()
    og.s5()
    for r, p in ORDER:
        og.recv_sibling(r, p)

    def output(first, count):
        r = pl.ds(first * QT, count * QT)

        def part(c, carry):
            cols = pl.ds(pl.multiple_of(c * 256, 256), 256)
            w = wo_all[:, :, :, cols].reshape(ctx_all.shape[1], 256)
            summed = jnp.dot(ctx_all[r, :], w, preferred_element_type=F32)
            mixed_v[r, cols] = (x_all[me_t, r, cols].astype(F32) + summed).astype(BF16)
            return carry

        lax.fori_loop(0, mixed_v.shape[1] // 256, part, 0)
        c = pltpu.make_async_copy(mixed_v.at[r], mixed.at[r], local_sem.at[6 + first])
        c.start()
        return c

    cg[0].s4_halves()
    cg[0].s5()
    puts = [put, output(0, 2)]
    for i in (1, 2):
        cg[i].s4_halves()
        cg[i].s5()
    puts.append(output(2, 2))
    for c in puts:
        c.wait()
    for i, (r, p) in enumerate(ORDER[1:]):
        spread_copy(i, k, moved(k, y=r, zl=p)).wait_send()
        settle_copy(i, k, moved(k, x=r, zh=p)).wait_send()
        ssq_copy(i, k, moved(k, x=r, zh=p)).wait_send()
    for i, (r, p, c) in enumerate(s_list):
        pos_copy(i, k, moved(k, y=r, zl=p, c=c)).wait_send()
    for x in [xg, wg, kg, og, *cg]:
        x.finish()


def shards(tokens, positions, norm_gain, w_query, w_key, w_value, b_query, b_key, b_value, w_out):
    rows, feats = tokens.shape
    qc, kc = w_query.shape[1], w_key.shape[1]
    wrows = w_query.shape[0]
    heads = qc // HD
    nt, ns = lax.axis_size("tensor"), lax.axis_size("seq")
    half = HD // 2
    inv_freq = ROPE_BASE ** (-jnp.arange(half, dtype=F32) * 2.0 / HD)
    angles = positions.astype(F32)[:, None] * inv_freq[None, :]
    cos, sin = jnp.cos(angles), jnp.sin(angles)
    cosine = jnp.concatenate([cos, cos], 1)
    sine = jnp.concatenate([-sin, sin], 1)
    bias = jnp.concatenate((b_query, b_key, b_value))[None, :]
    pos = jnp.pad(positions.astype(F32).reshape(rows // 128, 128), ((0, 8 - rows // 128), (0, 0)))
    any_, vmem = pl.BlockSpec(memory_space=pl.ANY), pl.BlockSpec(memory_space=pltpu.VMEM)
    dma = pltpu.SemaphoreType.DMA
    return pl.pallas_call(
        block_kernel,
        name="block",
        out_shape=(
            jax.ShapeDtypeStruct((rows, feats), BF16),
            jax.ShapeDtypeStruct((rows, qc), BF16),
        ),
        in_specs=[any_, any_, vmem, any_, any_, any_, vmem, vmem, vmem, any_],
        out_specs=(any_, any_),
        scratch_shapes=[
            pltpu.VMEM((nt, rows, feats), BF16),
            pltpu.VMEM((ns, wrows, qc + 2 * kc), BF16),
            pltpu.VMEM((rows, qc + 2 * kc), F32),
            pltpu.VMEM((rows, feats), BF16),
            pltpu.VMEM((nt, 8, 128), F32),
            pltpu.VMEM((rows, 128), F32),
            pltpu.VMEM((nt, w_out.shape[0] // 8, w_out.shape[1]), BF16),
            pltpu.VMEM((ns, 8, 128), F32),
            pltpu.VMEM((heads, rows, HD), BF16),
            pltpu.VMEM((ns * rows, 2 * HD), BF16),
            pltpu.VMEM((nt, 8, qc // 8, feats), BF16),
            pltpu.VMEM((rows, nt * qc), BF16),
            pltpu.VMEM((ns, 1, rows), F32),
            pltpu.VMEM((rows, 128), F32),
            pltpu.VMEM((heads, rows, 128), F32),
            pltpu.VMEM((heads, rows, 128), F32),
            pltpu.VMEM((heads, rows, HD), F32),
            pltpu.VMEM((rows, feats), BF16),
            dma((10,)), dma((20,)), dma((20,)), dma((20,)), dma((20,)),
            dma((8,)), dma((8,)), dma((16,)), dma((16,)), dma((16,)), dma((16,)),
            dma((20,)), dma((20,)), dma((20,)), dma((20,)), dma((48,)), dma((48,)),
        ],
        compiler_params=pltpu.CompilerParams(
            collective_id=0, has_side_effects=True, vmem_limit_bytes=62 * 1024 * 1024
        ),
    )(tokens, pos, norm_gain.reshape(nt, 1, feats), w_query, w_key, w_value, bias, cosine, sine, w_out)


def solution(mesh):
    in_specs = (
        P("seq", "tensor"),
        P("seq"),
        P(),
        P("seq", "tensor"),
        P("seq", "tensor"),
        P("seq", "tensor"),
        P("tensor"),
        P("tensor"),
        P("tensor"),
        P("tensor", "seq"),
    )
    out_specs = (P("seq", "tensor"), P("seq", "tensor"))
    return jax.shard_map(shards, mesh=mesh, in_specs=in_specs, out_specs=out_specs, check_vma=False)
```

time: 227 us -> 172 us (0.76)
  Pallas kernels: 218 us -> 163 us
    pallas_call x2 -> x1, Pallas kernels: 218 us -> 163 us  [shards(): pl.pallas_call(block_kernel, name='block', out_shape=(jax.ShapeDtypeStruc...]
    unnamed x22 -> x12, local copies, waits for them, and re-layouts: 5.89 us -> 3.85 us
where the time goes in v2:
time: 172 us; the launch traced here: 171 us
  Pallas kernels  163 us (95%)
  local copies, waits for them, and re-layouts  5.03 us (3%)
  other arithmetic  2.01 us (1%)
    pallas_call x1, Pallas kernels, shards(): pl.pallas_call(block_kernel, name='block', out_shape=(jax.ShapeDtypeStruc...  163 us
    unnamed x12, local copies, waits for them, and re-layouts  3.85 us

profile of v2, /device:TPU:0, one launch (start us, length us, event | category | flops | bytes accessed | tf_op | source)
XLA Modules:
  0.0 171.0 jit_solution(13238845884422735942)
XLA Ops:
  0.6 0.0 copy-start.1
  0.6 0.0 copy-start.3
  0.7 0.0 copy-start.4
  0.7 0.6 copy-done.1
  1.3 0.0 copy-done.3
  1.3 0.0 copy-done.4
  1.3 0.0 copy-start.2
  1.3 0.6 broadcast_in_dim.2.bias
  1.9 0.1 copy-done.2
  2.0 0.6 pad.4.pos
  2.6 1.0 fusion
  3.6 1.0 pad_maximum_fusion
  4.6 163.3 %block.1 = (bf16[512,1024]{1,0:T(8,128)(2,1)}, bf16[512,512]{1,0:T(8,128)(2,1)}) custom-call(bf16[512,1024]{1,0:T(8,128)(2,1)} %tokens.1, f32[8,128]{1,0:T(8,128)} %pad.4.pos, f32[8,1,1024]{2,1,0:T(1,128)} %bitcast.3, bf16[512,512]{1,0:T(8,128)(2,1)} %w_query.1, bf16[512,128]{1,0:T(8,128)(2,1)} %w_key.1, bf16[512,128]{1,0:T(8,128)(2,1)} %w_value.1, ...), custom_call_target="tpu_custom_call" | custom-call | tf_op jit(solution)/shard_map/block/pallas_call | solution.py:554
  167.9 0.0 copy-start
  167.9 2.3 %copy.14 = bf16[512,1024]{1,0:T(8,128)(2,1)} copy(bf16[512,1024]{1,0:T(8,128)(2,1)} %get-tuple-element.11) | data formatting | bytes 2097152
  170.2 0.0 copy-done
  170.2 0.8 copy.15
  (3 shorter events, 0.0 us)
Async XLA Ops:
  0.6 0.7 copy-start.1
  0.6 0.7 copy-start.3
  0.7 0.7 copy-start.4
  1.3 0.7 copy-start.2
  167.9 2.3 %copy-start = (bf16[512,512]{1,0:T(8,128)(2,1)S(1)}, bf16[512,512]{1,0:T(8,128)(2,1)}, u32[]{:S(2)}) copy-start(bf16[512,512]{1,0:T(8,128)(2,1)} %get-tuple-element.12) | copy-start | bytes 1572868

commit v3 on v2

--- a/solution.py
+++ b/solution.py
@@ -45,10 +45,11 @@
 
 
 class Gather:
-    def __init__(self, k, slot, half_rows, ring, pair, sibling, ssem, rsem, base=0):
+    def __init__(self, k, slot, half_rows, ring, pair, sibling, ssem, rsem, base=0, along=0):
         self.k, self.slot, self.half = k, slot, half_rows
         self.ring, self.pair, self.sibling = ring, pair, sibling
         self.ssem, self.rsem, self.base = ssem, rsem, base
+        self.along, self.direct = along, 2 * half_rows - 2 * along
         self.sent = []
 
     def at(self, r=0, p=0, c=0):
@@ -61,7 +62,8 @@
     def copy(self, i, block, target, half):
         ref = self.slot(self.place(block))
         if half is not None:
-            ref = ref.at[pl.ds(half * self.half, self.half)]
+            first, count = half if isinstance(half, tuple) else (half * self.half, self.half)
+            ref = ref.at[pl.ds(first, count)]
         return pltpu.make_async_remote_copy(
             src_ref=ref,
             dst_ref=ref,
@@ -90,6 +92,14 @@
             self.send(2, own, self.at(p=1))
         self.share(3, own)
 
+    def s0_ring(self):
+        self.send(0, self.at(), self.at(1))
+        self.send(1, self.at(), self.at(-1))
+        self.share(3, self.at())
+
+    def s0_pair(self):
+        self.send(2, self.at(), self.at(p=1))
+
     def pair_halves(self):
         self.send(2, self.at(), self.at(p=1), 0)
         self.send(3, self.at(), self.at(p=1), 1)
@@ -117,13 +127,16 @@
         for h in (0, 1):
             self.recv(8 + 2 * h, self.at(-1, 1), h)
             self.recv(9 + 2 * h, self.at(1, 1), h)
+        if self.along:
+            self.send(14, self.at(-1, 1), self.at(1), (self.direct, self.along))
+            self.send(15, self.at(1, 1), self.at(-1), (self.direct + self.along, self.along))
 
     def s3(self):
         self.recv(4, self.at(2), 0)
         self.recv(6, self.at(2), 1)
         self.share(11, self.at(2))
         if not self.sibling:
-            self.send(13, self.at(2), self.at(p=1))
+            self.send(13, self.at(2), self.at(p=1), (0, self.direct))
 
     def s4(self):
         self.recv(8, self.at(-1, 1))
@@ -141,7 +154,10 @@
             self.recv(15, self.at(2, 1), 1)
             self.share(17, self.at(2, 1))
         else:
-            self.recv(13, self.at(2, 1))
+            self.recv(13, self.at(2, 1), (0, self.direct))
+            if self.along:
+                self.recv(14, self.at(2, 1), (self.direct, self.along))
+                self.recv(15, self.at(2, 1), (self.direct + self.along, self.along))
 
     SHARED = {(0, 0): 3, (-1, 0): 5, (1, 0): 7, (0, 1): 10, (2, 0): 11, (-1, 1): 14, (1, 1): 16, (2, 1): 17}
 
@@ -188,13 +204,14 @@
 QT = 128
 CHUNKS = ((0, 2), (2, 1), (3, 1))
 GROUP = 2
+ALONG = 64
 
 
 def block_kernel(
     tokens, pos, gain, w_query, w_key, w_value, bias, cosine, sine, w_out,
     mixed, context,
     x_all, w_all, acc, normed, ssq, inverse, wo_mid, pos_all,
-    q, kv_all, wo_all, ctx_all, key_pos, own_pos, top, low, num, mixed_v,
+    q, kv_all, wo_all, ctx_all, key_pos, own_pos, top, low, num,
     local_sem, x_ssem, x_rsem, w_ssem, w_rsem, s_ssem, s_rsem, p_ssem, p_rsem, t_ssem, t_rsem,
     kv_ssem, kv_rsem, wo_ssem, wo_rsem, c_ssem, c_rsem,
 ):
@@ -227,7 +244,7 @@
             pl.ds(first * QT, count * QT), pl.ds(pl.multiple_of(tensor_of(b) * cw, cw), cw)
         ]
 
-    xg = Gather(k, lambda b: x_all.at[tensor_of(b)], rows // 2, "x", "zh", False, x_ssem, x_rsem)
+    xg = Gather(k, lambda b: x_all.at[tensor_of(b)], rows // 2, "x", "zh", False, x_ssem, x_rsem, along=ALONG)
     wg = Gather(k, lambda b: w_all.at[seq_of(b)], wrows // 2, "y", "zl", True, w_ssem, w_rsem)
     kg = Gather(
         k, lambda b: kv_all.at[pl.ds(pl.multiple_of(seq_of(b) * rows, rows), rows)], rows // 2,
@@ -328,7 +345,7 @@
     for i, (r, p) in enumerate(ORDER[1:]):
         settle_copy(i, moved(k, x=-r, zh=p), moved(k, x=r, zh=p)).wait_recv()
     settle_own.wait()
-    og.s0()
+    og.s0_ring()
     wg.s5()
     for r, p in ORDER:
         wg.recv_sibling(r, p)
@@ -374,6 +391,7 @@
     for h in range(heads):
         q[h] = turned(h)
     kg.s0()
+    og.s0_pair()
 
     factor = HD ** (-0.5) / math.log(2.0)
     keys = 2 * rows
@@ -391,28 +409,36 @@
         r = pl.ds(f * QT, n * QT)
         for h in range(heads):
             bottom = jnp.sum(low[h, r, :], -1, keepdims=True)
-            ctx_all[r, pl.ds(pl.multiple_of(me_t * cw + h * HD, HD), HD)] = (
-                num[h, r, :] / bottom
-            ).astype(BF16)
+            done = (num[h, r, :] / bottom).astype(BF16)
+            ctx_all[r, pl.ds(pl.multiple_of(me_t * cw + h * HD, HD), HD)] = done
+            context[r, h * HD : (h + 1) * HD] = done
 
     def send_ctx(i):
         cg[i].s0()
         cg[i].pair_halves()
 
+    def settle_sends():
+        for i, (r, p) in enumerate(ORDER[1:]):
+            spread_copy(i, k, moved(k, y=r, zl=p)).wait_send()
+            settle_copy(i, k, moved(k, x=r, zh=p)).wait_send()
+            ssq_copy(i, k, moved(k, x=r, zh=p)).wait_send()
+        for i, (r, p, c) in enumerate(s_list):
+            pos_copy(i, k, moved(k, y=r, zl=p, c=c)).wait_send()
+        xg.finish()
+        wg.finish()
+
     event(0, sib(0, 0))
-    event(4, kg.s1, sib(-1, 0))
-    event(5, kg.s2)
-    event(6, sib(1, 0))
-    event(8, sib(0, 1))
-    event(10, kg.s3, sib(2, 0))
-    event(12, kg.s4, sib(-1, 1), og.s1)
-    event(14, sib(1, 1))
-    event(16, kg.s5, sib(2, 1), og.s2)
-    event(18, lambda: close(0), lambda: send_ctx(0))
-    event(24, cg[0].s1)
-    event(25, lambda: close(1), lambda: send_ctx(1), lambda: cg[0].s2_half(0))
-    event(27, lambda: cg[0].s2_half(1))
-    event(29, cg[0].s3, og.s3)
+    event(2, kg.s1, sib(-1, 0))
+    event(3, kg.s2, settle_sends, sib(1, 0))
+    event(4, sib(0, 1))
+    event(5, kg.s3, sib(2, 0))
+    event(6, kg.s4, sib(-1, 1), og.s1)
+    event(7, sib(1, 1))
+    event(8, kg.s5, sib(2, 1), og.s2)
+    event(9, lambda: close(0), lambda: send_ctx(0))
+    event(12, cg[0].s1)
+    event(13, lambda: close(1), lambda: send_ctx(1), lambda: cg[0].s2_half(0), lambda: cg[0].s2_half(1))
+    event(14, cg[0].s3, og.s3)
 
     def step(g, carry):
         for at, fns in sorted(events.items()):
@@ -421,117 +447,103 @@
                 for fn in fns:
                     fn()
 
-        late = jnp.maximum(g - 18, 0)
-        mid = jnp.maximum(g - 4, 0)
-        kb = jnp.where(g < 4, 0, jnp.where(g < 18, 1 + mid // 2, 1 + late % 7))
-        tile = jnp.where(g < 4, g, jnp.where(g < 18, mid % 2, 2 + late // 7))
-        dy = pick(kb, [r % 4 for r, _ in ORDER])
-        dz = pick(kb, [p for _, p in ORDER])
-        chip = ((k["y"] + dy) % 4) * 2 + (k["zl"] + dz) % 2
-        kr = pl.ds(pl.multiple_of(chip * keys, keys), keys)
-        qr = pl.ds(pl.multiple_of(tile * QT, QT), QT)
-        mine = jnp.concatenate([own_pos[qr, :]] * GROUP, 0)
-        gr = GROUP * QT
-
-        def scores(u):
-            hs = slice(u * GROUP, (u + 1) * GROUP)
+        units = [Unit(2 * g + half, u) for half in range(2) for u in range(heads // GROUP)]
+        s, held = units[0].scores(), None
+        for i, unit in enumerate(units):
+            later = units[i + 1].scores() if i + 1 < len(units) else None
+            now = unit.soften(s)
+            if held is not None:
+                units[i - 1].collect(*held)
+            s, held = later, now
+        units[-1].collect(*held)
+        return carry
+
+    class Unit:
+        def __init__(self, g, u):
+            late = jnp.maximum(g - 18, 0)
+            mid = jnp.maximum(g - 4, 0)
+            kb = jnp.where(g < 4, 0, jnp.where(g < 18, 1 + mid // 2, 1 + late % 7))
+            tile = jnp.where(g < 4, g, jnp.where(g < 18, mid % 2, 2 + late // 7))
+            dy = pick(kb, [r % 4 for r, _ in ORDER])
+            dz = pick(kb, [p for _, p in ORDER])
+            self.chip = ((k["y"] + dy) % 4) * 2 + (k["zl"] + dz) % 2
+            self.kr = pl.ds(pl.multiple_of(self.chip * keys, keys), keys)
+            self.at = (slice(u * GROUP, (u + 1) * GROUP), pl.ds(pl.multiple_of(tile * QT, QT), QT), slice(None))
+            self.mine = jnp.concatenate([own_pos[self.at[1], :]] * GROUP, 0)
+
+        def scores(self):
             return lax.dot_general(
-                q[hs, qr, :].reshape(gr, HD), kv_all[kr, 0:HD], (((1,), (1,)), ((), ())),
+                q[self.at].reshape(GROUP * QT, HD), kv_all[self.kr, 0:HD], (((1,), (1,)), ((), ())),
                 preferred_element_type=F32,
             )
 
-        def soften(u, s):
-            hs = slice(u * GROUP, (u + 1) * GROUP)
+        def soften(self, s):
             parts = []
             for j in range(keys // 128):
-                at = (j % (rows // 128)) * 128
-                kp = key_pos[chip * 2 + j // (rows // 128), :, at : at + 128]
-                parts.append(jnp.where(kp <= mine, s[:, j * 128 : (j + 1) * 128], NEG_FILL))
+                lane = (j % (rows // 128)) * 128
+                kp = key_pos[self.chip * 2 + j // (rows // 128), :, lane : lane + 128]
+                parts.append(jnp.where(kp <= self.mine, s[:, j * 128 : (j + 1) * 128], NEG_FILL))
             best = parts[0]
             for x in parts[1:]:
                 best = jnp.maximum(best, x)
-            old = top[hs, qr, :].reshape(gr, 128)
+            old = top[self.at].reshape(GROUP * QT, 128)
             new = jnp.maximum(old, jnp.max(best, -1, keepdims=True))
-            top[hs, qr, :] = new.reshape(GROUP, QT, 128)
+            top[self.at] = new.reshape(GROUP, QT, 128)
             alpha = jnp.exp2((old - new) * factor)
-            weights, total = [], low[hs, qr, :].reshape(gr, 128) * alpha
+            weights, total = [], low[self.at].reshape(GROUP * QT, 128) * alpha
             for x in parts:
                 w = jnp.exp2((x - new) * factor)
                 total = total + w
                 weights.append(w.astype(BF16))
-            low[hs, qr, :] = total.reshape(GROUP, QT, 128)
+            low[self.at] = total.reshape(GROUP, QT, 128)
             return alpha, jnp.concatenate(weights, 1)
 
-        def collect(u, alpha, weights):
-            hs = slice(u * GROUP, (u + 1) * GROUP)
-            out = num[hs, qr, :].reshape(gr, HD) * alpha + jnp.dot(
-                weights, kv_all[kr, HD : 2 * HD], preferred_element_type=F32
+        def collect(self, alpha, weights):
+            out = num[self.at].reshape(GROUP * QT, HD) * alpha + jnp.dot(
+                weights, kv_all[self.kr, HD : 2 * HD], preferred_element_type=F32
             )
-            num[hs, qr, :] = out.reshape(GROUP, QT, HD)
-
-        units = heads // GROUP
-        s, held = scores(0), None
-        for u in range(units):
-            later = scores(u + 1) if u + 1 < units else None
-            now = soften(u, s)
-            if held is not None:
-                collect(u - 1, *held)
-            s, held = later, now
-        collect(units - 1, *held)
-        return carry
-
-    lax.fori_loop(0, 8 * tiles, step, 0)
+            num[self.at] = out.reshape(GROUP, QT, HD)
+
+    lax.fori_loop(0, 4 * tiles, step, 0)
 
     close(2)
     send_ctx(2)
-    put = pltpu.make_async_copy(
-        ctx_all.at[:, pl.ds(pl.multiple_of(me_t * cw, cw), cw)], context, local_sem.at[5]
-    )
-    put.start()
+    def output(first, count):
+        r = pl.ds(first * QT, count * QT)
+
+        def part(c, carry):
+            cols = pl.ds(pl.multiple_of(c * 256, 256), 256)
+            w = wo_all[:, :, :, cols].reshape(ctx_all.shape[1], 256)
+            summed = jnp.dot(ctx_all[r, :], w, preferred_element_type=F32)
+            mixed[r, cols] = (x_all[me_t, r, cols].astype(F32) + summed).astype(BF16)
+            return carry
+
+        lax.fori_loop(0, mixed.shape[1] // 256, part, 0)
+
     cg[1].s1()
     cg[1].s2_half(0)
     cg[1].s2_half(1)
     og.s4()
+    og.s5()
+    for r, p in ORDER:
+        og.recv_sibling(r, p)
+    cg[0].s4_halves()
+    cg[0].s5()
     cg[1].s3()
     cg[2].s1()
     cg[2].s2_half(0)
     cg[2].s2_half(1)
+    output(0, 2)
     cg[2].s3()
-    og.s5()
-    for r, p in ORDER:
-        og.recv_sibling(r, p)
-
-    def output(first, count):
-        r = pl.ds(first * QT, count * QT)
-
-        def part(c, carry):
-            cols = pl.ds(pl.multiple_of(c * 256, 256), 256)
-            w = wo_all[:, :, :, cols].reshape(ctx_all.shape[1], 256)
-            summed = jnp.dot(ctx_all[r, :], w, preferred_element_type=F32)
-            mixed_v[r, cols] = (x_all[me_t, r, cols].astype(F32) + summed).astype(BF16)
-            return carry
-
-        lax.fori_loop(0, mixed_v.shape[1] // 256, part, 0)
-        c = pltpu.make_async_copy(mixed_v.at[r], mixed.at[r], local_sem.at[6 + first])
-        c.start()
-        return c
-
-    cg[0].s4_halves()
-    cg[0].s5()
-    puts = [put, output(0, 2)]
-    for i in (1, 2):
-        cg[i].s4_halves()
-        cg[i].s5()
-    puts.append(output(2, 2))
-    for c in puts:
-        c.wait()
-    for i, (r, p) in enumerate(ORDER[1:]):
-        spread_copy(i, k, moved(k, y=r, zl=p)).wait_send()
-        settle_copy(i, k, moved(k, x=r, zh=p)).wait_send()
-        ssq_copy(i, k, moved(k, x=r, zh=p)).wait_send()
-    for i, (r, p, c) in enumerate(s_list):
-        pos_copy(i, k, moved(k, y=r, zl=p, c=c)).wait_send()
-    for x in [xg, wg, kg, og, *cg]:
+    cg[1].s4_halves()
+    cg[1].s5()
+    output(2, 1)
+    kg.finish()
+    og.finish()
+    cg[2].s4_halves()
+    cg[2].s5()
+    output(3, 1)
+    for x in cg:
         x.finish()
 
 
@@ -549,7 +561,7 @@
     sine = jnp.concatenate([-sin, sin], 1)
     bias = jnp.concatenate((b_query, b_key, b_value))[None, :]
     pos = jnp.pad(positions.astype(F32).reshape(rows // 128, 128), ((0, 8 - rows // 128), (0, 0)))
-    any_, vmem = pl.BlockSpec(memory_space=pl.ANY), pl.BlockSpec(memory_space=pltpu.VMEM)
+    any_, vmem = pl.BlockSpec(memory_space=pltpu.HBM), pl.BlockSpec(memory_space=pltpu.VMEM)
     dma = pltpu.SemaphoreType.DMA
     return pl.pallas_call(
         block_kernel,
@@ -559,7 +571,7 @@
             jax.ShapeDtypeStruct((rows, qc), BF16),
         ),
         in_specs=[any_, any_, vmem, any_, any_, any_, vmem, vmem, vmem, any_],
-        out_specs=(any_, any_),
+        out_specs=(vmem, vmem),
         scratch_shapes=[
             pltpu.VMEM((nt, rows, feats), BF16),
             pltpu.VMEM((ns, wrows, qc + 2 * kc), BF16),
@@ -578,13 +590,12 @@
             pltpu.VMEM((heads, rows, 128), F32),
             pltpu.VMEM((heads, rows, 128), F32),
             pltpu.VMEM((heads, rows, HD), F32),
-            pltpu.VMEM((rows, feats), BF16),
             dma((10,)), dma((20,)), dma((20,)), dma((20,)), dma((20,)),
             dma((8,)), dma((8,)), dma((16,)), dma((16,)), dma((16,)), dma((16,)),
             dma((20,)), dma((20,)), dma((20,)), dma((20,)), dma((48,)), dma((48,)),
         ],
         compiler_params=pltpu.CompilerParams(
-            collective_id=0, has_side_effects=True, vmem_limit_bytes=62 * 1024 * 1024
+            collective_id=0, has_side_effects=True, vmem_limit_bytes=56 * 1024 * 1024
         ),
     )(tokens, pos, norm_gain.reshape(nt, 1, feats), w_query, w_key, w_value, bias, cosine, sine, w_out)
 

time: 172 us -> 162 us (0.942)
  Pallas kernels: 163 us -> 154 us
    pallas_call x1, Pallas kernels: 163 us -> 154 us  [shards(): pl.pallas_call(block_kernel, name='block', out_shape=(jax.ShapeDtypeStruc...]
where the time goes in v3:
time: 162 us; the launch traced here: 161 us
  Pallas kernels  154 us (95%)
  local copies, waits for them, and re-layouts  5.03 us (3%)
  other arithmetic  2.01 us (1%)
    pallas_call x1, Pallas kernels, shards(): pl.pallas_call(block_kernel, name='block', out_shape=(jax.ShapeDtypeStruc...  154 us
    unnamed x12, local copies, waits for them, and re-layouts  3.85 us

profile of v3, /device:TPU:0, one launch (start us, length us, event | category | flops | bytes accessed | tf_op | source)
XLA Modules:
  0.0 161.3 jit_solution(9972499218817298328)
XLA Ops:
  0.6 0.0 copy-start.1
  0.6 0.0 copy-start.3
  0.7 0.0 copy-start.4
  0.7 0.6 copy-done.1
  1.3 0.0 copy-done.3
  1.3 0.0 copy-done.4
  1.3 0.0 copy-start.2
  1.3 0.6 broadcast_in_dim.2.bias
  1.9 0.1 copy-done.2
  2.0 0.6 pad.4.pos
  2.6 1.0 fusion
  3.6 1.0 pad_maximum_fusion
  4.6 153.6 %block.1 = (bf16[512,1024]{1,0:T(8,128)(2,1)}, bf16[512,512]{1,0:T(8,128)(2,1)}) custom-call(bf16[512,1024]{1,0:T(8,128)(2,1)} %tokens.1, f32[8,128]{1,0:T(8,128)} %pad.4.pos, f32[8,1,1024]{2,1,0:T(1,128)} %bitcast.3, bf16[512,512]{1,0:T(8,128)(2,1)} %w_query.1, bf16[512,128]{1,0:T(8,128)(2,1)} %w_key.1, bf16[512,128]{1,0:T(8,128)(2,1)} %w_value.1, ...), custom_call_target="tpu_custom_call" | custom-call | tf_op jit(solution)/shard_map/block/pallas_call | solution.py:566
  158.2 0.0 copy-start
  158.2 2.3 %copy.14 = bf16[512,1024]{1,0:T(8,128)(2,1)} copy(bf16[512,1024]{1,0:T(8,128)(2,1)} %get-tuple-element.11) | data formatting | bytes 2097152
  160.5 0.0 copy-done
  160.5 0.8 copy.15
  (3 shorter events, 0.0 us)
Async XLA Ops:
  0.6 0.7 copy-start.1
  0.6 0.7 copy-start.3
  0.7 0.7 copy-start.4
  1.3 0.7 copy-start.2
  158.2 2.3 %copy-start = (bf16[512,512]{1,0:T(8,128)(2,1)S(1)}, bf16[512,512]{1,0:T(8,128)(2,1)}, u32[]{:S(2)}) copy-start(bf16[512,512]{1,0:T(8,128)(2,1)} %get-tuple-element.12) | copy-start | bytes 1572868

commit v4 on v3

--- a/solution.py
+++ b/solution.py
@@ -45,11 +45,12 @@
 
 
 class Gather:
-    def __init__(self, k, slot, half_rows, ring, pair, sibling, ssem, rsem, base=0, along=0):
+    def __init__(self, k, slot, half_rows, ring, pair, sibling, ssem, rsem, base=0, along=0, far_by_pair=False):
         self.k, self.slot, self.half = k, slot, half_rows
         self.ring, self.pair, self.sibling = ring, pair, sibling
         self.ssem, self.rsem, self.base = ssem, rsem, base
         self.along, self.direct = along, 2 * half_rows - 2 * along
+        self.far_by_pair = far_by_pair or not sibling
         self.sent = []
 
     def at(self, r=0, p=0, c=0):
@@ -85,12 +86,8 @@
             self.send(i, block, self.at(c=1))
 
     def s0(self):
-        own = self.at()
-        self.send(0, own, self.at(1))
-        self.send(1, own, self.at(-1))
-        if self.sibling:
-            self.send(2, own, self.at(p=1))
-        self.share(3, own)
+        self.s0_ring()
+        self.s0_pair()
 
     def s0_ring(self):
         self.send(0, self.at(), self.at(1))
@@ -99,10 +96,6 @@
 
     def s0_pair(self):
         self.send(2, self.at(), self.at(p=1))
-
-    def pair_halves(self):
-        self.send(2, self.at(), self.at(p=1), 0)
-        self.send(3, self.at(), self.at(p=1), 1)
 
     def s1(self):
         self.recv(0, self.at(-1))
@@ -118,46 +111,37 @@
         self.send(9, self.at(p=1), self.at(-1))
         self.share(10, self.at(p=1))
 
-    def s2_half(self, h):
-        self.recv(2 + h, self.at(p=1), h)
-        self.send(8 + 2 * h, self.at(p=1), self.at(1), h)
-        self.send(9 + 2 * h, self.at(p=1), self.at(-1), h)
-
-    def s4_halves(self):
-        for h in (0, 1):
-            self.recv(8 + 2 * h, self.at(-1, 1), h)
-            self.recv(9 + 2 * h, self.at(1, 1), h)
-        if self.along:
-            self.send(14, self.at(-1, 1), self.at(1), (self.direct, self.along))
-            self.send(15, self.at(1, 1), self.at(-1), (self.direct + self.along, self.along))
-
     def s3(self):
         self.recv(4, self.at(2), 0)
         self.recv(6, self.at(2), 1)
         self.share(11, self.at(2))
-        if not self.sibling:
+        if self.far_by_pair:
             self.send(13, self.at(2), self.at(p=1), (0, self.direct))
 
     def s4(self):
         self.recv(8, self.at(-1, 1))
-        if self.sibling:
+        if not self.far_by_pair:
             self.send(13, self.at(-1, 1), self.at(1), 0)
+        elif self.along:
+            self.send(14, self.at(-1, 1), self.at(1), (self.direct, self.along))
         self.share(14, self.at(-1, 1))
         self.recv(9, self.at(1, 1))
-        if self.sibling:
+        if not self.far_by_pair:
             self.send(15, self.at(1, 1), self.at(-1), 1)
+        elif self.along:
+            self.send(15, self.at(1, 1), self.at(-1), (self.direct + self.along, self.along))
         self.share(16, self.at(1, 1))
 
     def s5(self):
-        if self.sibling:
-            self.recv(13, self.at(2, 1), 0)
-            self.recv(15, self.at(2, 1), 1)
-            self.share(17, self.at(2, 1))
-        else:
+        if self.far_by_pair:
             self.recv(13, self.at(2, 1), (0, self.direct))
             if self.along:
                 self.recv(14, self.at(2, 1), (self.direct, self.along))
                 self.recv(15, self.at(2, 1), (self.direct + self.along, self.along))
+        else:
+            self.recv(13, self.at(2, 1), 0)
+            self.recv(15, self.at(2, 1), 1)
+        self.share(17, self.at(2, 1))
 
     SHARED = {(0, 0): 3, (-1, 0): 5, (1, 0): 7, (0, 1): 10, (2, 0): 11, (-1, 1): 14, (1, 1): 16, (2, 1): 17}
 
@@ -204,14 +188,14 @@
 QT = 128
 CHUNKS = ((0, 2), (2, 1), (3, 1))
 GROUP = 2
-ALONG = 64
+ALONG = (64, 0)
 
 
 def block_kernel(
     tokens, pos, gain, w_query, w_key, w_value, bias, cosine, sine, w_out,
     mixed, context,
     x_all, w_all, acc, normed, ssq, inverse, wo_mid, pos_all,
-    q, kv_all, wo_all, ctx_all, key_pos, own_pos, top, low, num,
+    q, kv_all, wo_all, ctx_all, key_pos, own_pos, top, low, num, mixed_v,
     local_sem, x_ssem, x_rsem, w_ssem, w_rsem, s_ssem, s_rsem, p_ssem, p_rsem, t_ssem, t_rsem,
     kv_ssem, kv_rsem, wo_ssem, wo_rsem, c_ssem, c_rsem,
 ):
@@ -244,13 +228,28 @@
             pl.ds(first * QT, count * QT), pl.ds(pl.multiple_of(tensor_of(b) * cw, cw), cw)
         ]
 
-    xg = Gather(k, lambda b: x_all.at[tensor_of(b)], rows // 2, "x", "zh", False, x_ssem, x_rsem, along=ALONG)
+    part_rows = rows // 2
+    xg = [
+        Gather(
+            k, lambda b, h=h: x_all.at[tensor_of(b), pl.ds(h * part_rows, part_rows)], part_rows // 2,
+            "x", "zh", False, x_ssem, x_rsem, base=20 * h, along=ALONG[h],
+        )
+        for h in range(2)
+    ]
     wg = Gather(k, lambda b: w_all.at[seq_of(b)], wrows // 2, "y", "zl", True, w_ssem, w_rsem)
-    kg = Gather(
-        k, lambda b: kv_all.at[pl.ds(pl.multiple_of(seq_of(b) * rows, rows), rows)], rows // 2,
-        "y", "zl", True, kv_ssem, kv_rsem,
+    def kv_rows(h, b):
+        return pl.ds(pl.multiple_of((h * 16 + seq_of(b)) * part_rows, part_rows), part_rows)
+
+    kg = [
+        Gather(
+            k, lambda b, h=h: kv_all.at[kv_rows(h, b)], part_rows // 2, "y", "zl", True,
+            kv_ssem, kv_rsem, base=20 * h, far_by_pair=h == 1,
+        )
+        for h in range(2)
+    ]
+    og = Gather(
+        k, wo_slot, wo_all.shape[0] // 2, "y", "zl", True, wo_ssem, wo_rsem
     )
-    og = Gather(k, wo_slot, wo_all.shape[0] // 2, "y", "zl", True, wo_ssem, wo_rsem)
     cg = [
         Gather(k, ctx_slot(f, n), n * QT // 2, "x", "zh", False, c_ssem, c_rsem, base=16 * i)
         for i, (f, n) in enumerate(CHUNKS)
@@ -293,14 +292,12 @@
         )
 
     wg.s0()
-    xg.s0()
+    xg[0].s0_ring()
+    xg[1].s0_ring()
     for i in range(rows // 128):
         xb = x_all[me_t, pl.ds(i * 128, 128), :].astype(F32)
         total = jnp.sum(xb * xb, -1, keepdims=True)
         ssq[me_t, i : i + 1, :] = jnp.broadcast_to(total, (128, 128)).T[0:1, :]
-    for i, (r, p) in enumerate(ORDER[1:]):
-        spread_copy(i, k, moved(k, y=r, zl=p)).start()
-    spread_own.start()
     for i, (r, p, c) in enumerate(s_list):
         pos_copy(i, k, moved(k, y=r, zl=p, c=c)).start()
     acc[...] = jnp.zeros_like(acc)
@@ -312,8 +309,9 @@
 
     wg.s1()
     wg.s2()
-    xg.pair_halves()
-    xg.s1()
+    xg[0].s0_pair()
+    xg[0].s1()
+    xg[1].s1()
     for i, (r, p) in enumerate(ORDER[1:]):
         ssq_copy(i, moved(k, x=-r, zh=p), k).wait_recv()
     total = ssq[0]
@@ -322,76 +320,102 @@
     scale = lax.rsqrt(total / (8 * x_all.shape[2]) + NORM_EPS)
     inverse[...] = as_columns(scale[0 : rows // 128, :])
     wg.s3()
-    xg.s2_half(0)
+    xg[0].s3()
+    xg[1].s0_pair()
+    xg[0].s2()
+    xg[1].s3()
+    wg.s4()
     for i, (r, p) in enumerate(ORDER[1:]):
-        spread_copy(i, moved(k, y=-r, zl=p), moved(k, y=r, zl=p)).wait_recv()
-    spread_own.wait()
-    for i, (r, p) in enumerate(ORDER[1:]):
-        settle_copy(i, k, moved(k, x=r, zh=p)).start()
-    settle_own.start()
-    xg.s3()
-    xg.s2_half(1)
-    wg.s4()
+        spread_copy(i, k, moved(k, y=r, zl=p)).start()
+    spread_own.start()
+    xg[0].s4()
+    xg[1].s2()
     for i, (r, p, c) in enumerate(s_list):
         pos_copy(i, moved(k, y=-r, zl=p, c=c), k).wait_recv()
 
     def spread(s, carry):
-        for j in range(rows // 128):
-            key_pos[s, :, j * 128 : (j + 1) * 128] = pos_all[s, j : j + 1, :]
+        for h in range(2):
+            for j in range(part_rows // 128):
+                row = h * (part_rows // 128) + j
+                key_pos[h * 16 + s, :, j * 128 : (j + 1) * 128] = pos_all[s, row : row + 1, :]
         return carry
 
     lax.fori_loop(0, pos_all.shape[0], spread, 0)
     own_pos[...] = as_columns(pos_all[me_s][0 : rows // 128, :])
-    for i, (r, p) in enumerate(ORDER[1:]):
-        settle_copy(i, moved(k, x=-r, zh=p), moved(k, x=r, zh=p)).wait_recv()
-    settle_own.wait()
-    og.s0_ring()
+    def settle():
+        for i, (r, p) in enumerate(ORDER[1:]):
+            spread_copy(i, moved(k, y=-r, zl=p), moved(k, y=r, zl=p)).wait_recv()
+        spread_own.wait()
+        for i, (r, p) in enumerate(ORDER[1:]):
+            settle_copy(i, k, moved(k, x=r, zh=p)).start()
+        settle_own.start()
+
+    def settled():
+        for i, (r, p) in enumerate(ORDER[1:]):
+            settle_copy(i, moved(k, x=-r, zh=p), moved(k, x=r, zh=p)).wait_recv()
+        settle_own.wait()
+
     wg.s5()
     for r, p in ORDER:
         wg.recv_sibling(r, p)
 
-    def block(step, carry):
-        @pl.when(step == 5)
-        def _():
-            xg.s4_halves()
-
-        @pl.when(step == 7)
-        def _():
-            xg.s5()
-
-        dx = pick(step, [r % 4 for r, _ in ORDER])
-        dz = pick(step, [p for _, p in ORDER])
-        t = ((k["zh"] + dz) % 2) * 4 + (k["x"] + dx) % 4
-        g = gain[t]
-        for i in range(rows // 128):
-            inv = inverse[pl.ds(i * 128, 128), :]
-            for j in range(x_all.shape[2] // 128):
-                piece = x_all[t, pl.ds(i * 128, 128), pl.ds(j * 128, 128)].astype(F32)
-                normed[pl.ds(i * 128, 128), pl.ds(j * 128, 128)] = (
-                    piece * inv * g[:, j * 128 : (j + 1) * 128]
-                ).astype(BF16)
-        part = jnp.dot(normed[:, 0:wrows], w_all[2 * t], preferred_element_type=F32)
-        part = part + jnp.dot(
-            normed[:, wrows : 2 * wrows], w_all[2 * t + 1], preferred_element_type=F32
-        )
-        acc[...] += part
-        return carry
-
-    lax.fori_loop(0, 8, block, 0)
-
-    cos, sin = cosine[...], sine[...]
-    mine_r = pl.ds(pl.multiple_of(me_s * rows, rows), rows)
-
-    def turned(h):
-        u = acc[:, h * HD : (h + 1) * HD] + bias[:, h * HD : (h + 1) * HD]
-        return (u * cos + pltpu.roll(u, HD // 2, 1) * sin).astype(BF16)
-
-    kv_all[mine_r, 0:HD] = turned(heads)
-    kv_all[mine_r, HD : 2 * HD] = (acc[:, qc + kc :] + bias[:, qc + kc :]).astype(BF16)
-    for h in range(heads):
-        q[h] = turned(h)
-    kg.s0()
-    og.s0_pair()
+    cos_sin = (cosine, sine)
+
+    def project(h):
+        first = h * part_rows
+
+        def block(step, carry):
+            if h == 1:
+
+                @pl.when(step == 5)
+                def _():
+                    xg[1].s4()
+
+                @pl.when(step == 7)
+                def _():
+                    kg[0].s1()
+                    kg[0].s2()
+                    xg[1].s5()
+                    settle()
+
+            dx = pick(step, [r % 4 for r, _ in ORDER])
+            dz = pick(step, [p for _, p in ORDER])
+            t = ((k["zh"] + dz) % 2) * 4 + (k["x"] + dx) % 4
+            g = gain[t]
+            for i in range(part_rows // 128):
+                r = pl.ds(first + i * 128, 128)
+                inv = inverse[r, :]
+                for j in range(x_all.shape[2] // 128):
+                    piece = x_all[t, r, pl.ds(j * 128, 128)].astype(F32)
+                    normed[pl.ds(i * 128, 128), pl.ds(j * 128, 128)] = (
+                        piece * inv * g[:, j * 128 : (j + 1) * 128]
+                    ).astype(BF16)
+            part = jnp.dot(normed[:, 0:wrows], w_all[2 * t], preferred_element_type=F32)
+            part = part + jnp.dot(
+                normed[:, wrows : 2 * wrows], w_all[2 * t + 1], preferred_element_type=F32
+            )
+            acc[first : first + part_rows, :] += part
+            return carry
+
+        lax.fori_loop(0, 8, block, 0)
+        r = slice(first, first + part_rows)
+        cos, sin = (x[r, :] for x in cos_sin)
+
+        def turned(head):
+            u = acc[r, head * HD : (head + 1) * HD] + bias[:, head * HD : (head + 1) * HD]
+            return (u * cos + pltpu.roll(u, HD // 2, 1) * sin).astype(BF16)
+
+        own = kv_rows(h, k)
+        kv_all[own, 0:HD] = turned(heads)
+        kv_all[own, HD : 2 * HD] = (acc[r, qc + kc :] + bias[:, qc + kc :]).astype(BF16)
+        for head in range(heads):
+            q[head, r, :] = turned(head)
+
+    xg[0].s5()
+    project(0)
+    kg[0].s0()
+    project(1)
+    kg[1].s0()
 
     factor = HD ** (-0.5) / math.log(2.0)
     keys = 2 * rows
@@ -401,8 +425,8 @@
     def event(step, *fns):
         events.setdefault(step, []).extend(fns)
 
-    def sib(r, p):
-        return lambda: kg.recv_sibling(r, p)
+    def sib(h, r):
+        return lambda: (kg[h].recv_sibling(r, 0), kg[h].recv_sibling(r, 1))
 
     def close(i):
         f, n = CHUNKS[i]
@@ -411,11 +435,9 @@
             bottom = jnp.sum(low[h, r, :], -1, keepdims=True)
             done = (num[h, r, :] / bottom).astype(BF16)
             ctx_all[r, pl.ds(pl.multiple_of(me_t * cw + h * HD, HD), HD)] = done
-            context[r, h * HD : (h + 1) * HD] = done
 
     def send_ctx(i):
         cg[i].s0()
-        cg[i].pair_halves()
 
     def settle_sends():
         for i, (r, p) in enumerate(ORDER[1:]):
@@ -424,29 +446,39 @@
             ssq_copy(i, k, moved(k, x=r, zh=p)).wait_send()
         for i, (r, p, c) in enumerate(s_list):
             pos_copy(i, k, moved(k, y=r, zl=p, c=c)).wait_send()
-        xg.finish()
-        wg.finish()
+        for x in [*xg, wg]:
+            x.finish()
+
+    def ctx_last(i):
+        cg[i].s4()
+        cg[i].s5()
 
     event(0, sib(0, 0))
-    event(2, kg.s1, sib(-1, 0))
-    event(3, kg.s2, settle_sends, sib(1, 0))
-    event(4, sib(0, 1))
-    event(5, kg.s3, sib(2, 0))
-    event(6, kg.s4, sib(-1, 1), og.s1)
-    event(7, sib(1, 1))
-    event(8, kg.s5, sib(2, 1), og.s2)
+    event(2, kg[0].s3, kg[0].s4, sib(0, -1))
+    event(3, kg[1].s1, kg[1].s2, sib(0, 1))
+    event(4, settled, og.s0_ring, sib(1, 0), kg[0].s5)
+    event(5, kg[1].s3, og.s0_pair, sib(0, 2))
+    event(6, kg[1].s4, sib(1, -1))
+    event(7, sib(1, 1), settle_sends)
+    event(8, kg[1].s5, sib(1, 2))
     event(9, lambda: close(0), lambda: send_ctx(0))
-    event(12, cg[0].s1)
-    event(13, lambda: close(1), lambda: send_ctx(1), lambda: cg[0].s2_half(0), lambda: cg[0].s2_half(1))
-    event(14, cg[0].s3, og.s3)
+    event(11, og.s1)
+    event(13, og.s2, cg[0].s1, lambda: close(1), lambda: send_ctx(1))
+    event(14, cg[0].s2, og.s3)
+    event(15, cg[0].s3)
+
+    def dispatch(g, first, last):
+        if last - first == 1:
+            for fn in events.get(first, []):
+                fn()
+            return
+        middle = (first + last) // 2
+        lax.cond(
+            g < middle, lambda: dispatch(g, first, middle), lambda: dispatch(g, middle, last)
+        )
 
     def step(g, carry):
-        for at, fns in sorted(events.items()):
-            @pl.when(g == at)
-            def _(fns=fns):
-                for fn in fns:
-                    fn()
-
+        dispatch(g, 0, 4 * tiles)
         units = [Unit(2 * g + half, u) for half in range(2) for u in range(heads // GROUP)]
         s, held = units[0].scores(), None
         for i, unit in enumerate(units):
@@ -466,8 +498,8 @@
             tile = jnp.where(g < 4, g, jnp.where(g < 18, mid % 2, 2 + late // 7))
             dy = pick(kb, [r % 4 for r, _ in ORDER])
             dz = pick(kb, [p for _, p in ORDER])
-            self.chip = ((k["y"] + dy) % 4) * 2 + (k["zl"] + dz) % 2
-            self.kr = pl.ds(pl.multiple_of(self.chip * keys, keys), keys)
+            self.block = dz * 4 + (k["y"] + dy) % 4
+            self.kr = pl.ds(pl.multiple_of(self.block * keys, keys), keys)
             self.at = (slice(u * GROUP, (u + 1) * GROUP), pl.ds(pl.multiple_of(tile * QT, QT), QT), slice(None))
             self.mine = jnp.concatenate([own_pos[self.at[1], :]] * GROUP, 0)
 
@@ -480,8 +512,8 @@
         def soften(self, s):
             parts = []
             for j in range(keys // 128):
-                lane = (j % (rows // 128)) * 128
-                kp = key_pos[self.chip * 2 + j // (rows // 128), :, lane : lane + 128]
+                lane = (j % (part_rows // 128)) * 128
+                kp = key_pos[self.block * 4 + j // (part_rows // 128), :, lane : lane + 128]
                 parts.append(jnp.where(kp <= self.mine, s[:, j * 128 : (j + 1) * 128], NEG_FILL))
             best = parts[0]
             for x in parts[1:]:
@@ -515,36 +547,40 @@
             cols = pl.ds(pl.multiple_of(c * 256, 256), 256)
             w = wo_all[:, :, :, cols].reshape(ctx_all.shape[1], 256)
             summed = jnp.dot(ctx_all[r, :], w, preferred_element_type=F32)
-            mixed[r, cols] = (x_all[me_t, r, cols].astype(F32) + summed).astype(BF16)
+            mixed_v[r, cols] = (x_all[me_t, r, cols].astype(F32) + summed).astype(BF16)
             return carry
 
         lax.fori_loop(0, mixed.shape[1] // 256, part, 0)
-
+        c = pltpu.make_async_copy(mixed_v.at[r], mixed.at[r], local_sem.at[6 + first])
+        c.start()
+        return c
+
+    put = pltpu.make_async_copy(
+        ctx_all.at[:, pl.ds(pl.multiple_of(me_t * cw, cw), cw)], context, local_sem.at[5]
+    )
+    put.start()
+    kg[0].finish()
+    kg[1].finish()
     cg[1].s1()
-    cg[1].s2_half(0)
-    cg[1].s2_half(1)
+    cg[1].s2()
+    cg[0].s4()
+    cg[1].s3()
+    cg[2].s1()
     og.s4()
+    cg[2].s2()
+    cg[0].s5()
+    cg[2].s3()
+    ctx_last(1)
     og.s5()
     for r, p in ORDER:
         og.recv_sibling(r, p)
-    cg[0].s4_halves()
-    cg[0].s5()
-    cg[1].s3()
-    cg[2].s1()
-    cg[2].s2_half(0)
-    cg[2].s2_half(1)
-    output(0, 2)
-    cg[2].s3()
-    cg[1].s4_halves()
-    cg[1].s5()
-    output(2, 1)
-    kg.finish()
-    og.finish()
-    cg[2].s4_halves()
-    cg[2].s5()
-    output(3, 1)
-    for x in cg:
+    puts = [put, output(0, 2)]
+    ctx_last(2)
+    puts.append(output(2, 2))
+    for x in [og, *cg]:
         x.finish()
+    for c in puts:
+        c.wait()
 
 
 def shards(tokens, positions, norm_gain, w_query, w_key, w_value, b_query, b_key, b_value, w_out):
@@ -571,12 +607,12 @@
             jax.ShapeDtypeStruct((rows, qc), BF16),
         ),
         in_specs=[any_, any_, vmem, any_, any_, any_, vmem, vmem, vmem, any_],
-        out_specs=(vmem, vmem),
+        out_specs=(pl.BlockSpec(memory_space=pl.ANY), pl.BlockSpec(memory_space=pl.ANY)),
         scratch_shapes=[
             pltpu.VMEM((nt, rows, feats), BF16),
             pltpu.VMEM((ns, wrows, qc + 2 * kc), BF16),
             pltpu.VMEM((rows, qc + 2 * kc), F32),
-            pltpu.VMEM((rows, feats), BF16),
+            pltpu.VMEM((rows // 2, feats), BF16),
             pltpu.VMEM((nt, 8, 128), F32),
             pltpu.VMEM((rows, 128), F32),
             pltpu.VMEM((nt, w_out.shape[0] // 8, w_out.shape[1]), BF16),
@@ -585,17 +621,18 @@
             pltpu.VMEM((ns * rows, 2 * HD), BF16),
             pltpu.VMEM((nt, 8, qc // 8, feats), BF16),
             pltpu.VMEM((rows, nt * qc), BF16),
-            pltpu.VMEM((ns, 1, rows), F32),
+            pltpu.VMEM((2 * ns, 1, rows // 2), F32),
             pltpu.VMEM((rows, 128), F32),
             pltpu.VMEM((heads, rows, 128), F32),
             pltpu.VMEM((heads, rows, 128), F32),
             pltpu.VMEM((heads, rows, HD), F32),
-            dma((10,)), dma((20,)), dma((20,)), dma((20,)), dma((20,)),
+            pltpu.VMEM((rows, feats), BF16),
+            dma((10,)), dma((40,)), dma((40,)), dma((20,)), dma((20,)),
             dma((8,)), dma((8,)), dma((16,)), dma((16,)), dma((16,)), dma((16,)),
-            dma((20,)), dma((20,)), dma((20,)), dma((20,)), dma((48,)), dma((48,)),
+            dma((40,)), dma((40,)), dma((20,)), dma((20,)), dma((48,)), dma((48,)),
         ],
         compiler_params=pltpu.CompilerParams(
-            collective_id=0, has_side_effects=True, vmem_limit_bytes=56 * 1024 * 1024
+            collective_id=0, has_side_effects=True, vmem_limit_bytes=50 * 1024 * 1024
         ),
     )(tokens, pos, norm_gain.reshape(nt, 1, feats), w_query, w_key, w_value, bias, cosine, sine, w_out)
 

time: 162 us -> 152 us (0.938); the launches traced: 161 us -> 149 us
  Pallas kernels: 154 us -> 143 us
    pallas_call x1, Pallas kernels: 154 us -> 143 us  [shards(): pl.pallas_call(block_kernel, name='block', out_shape=(jax.ShapeDtypeStruc...]
    unnamed x12 -> x20, local copies, waits for them, and re-layouts: 3.85 us -> 4.1 us
where the time goes in v4:
time: 152 us; the launch traced here: 149 us
  Pallas kernels  143 us (94%)
  local copies, waits for them, and re-layouts  4.11 us (3%)
    pallas_call x1, Pallas kernels, shards(): pl.pallas_call(block_kernel, name='block', out_shape=(jax.ShapeDtypeStruc...  143 us
    unnamed x20, local copies, waits for them, and re-layouts  4.1 us

profile of v4, /device:TPU:0, one launch (start us, length us, event | category | flops | bytes accessed | tf_op | source)
XLA Modules:
  0.0 149.2 jit_solution(14450113298102726476)
XLA Ops:
  0.6 0.0 copy-start.5
  0.6 0.0 copy-start.7
  0.7 0.0 copy-start.8
  0.7 0.6 copy-done.5
  1.3 0.0 copy-done.7
  1.3 0.0 copy-done.8
  1.3 0.0 copy-start.6
  1.4 0.7 copy-done.6
  2.0 0.0 copy-start.4
  2.0 1.0 fusion
  3.0 0.0 copy-start
  3.0 0.0 copy-start.1
  3.0 0.0 copy-start.2
  3.1 0.0 copy-start.3
  3.1 0.2 pad_maximum_fusion
  3.3 0.0 copy-done.4
  3.3 0.8 copy-done
  4.1 0.2 copy-done.1
  4.2 0.0 copy-done.2
  4.2 0.0 copy-done.3
  4.3 143.2 %block.1 = (bf16[512,1024]{1,0:T(8,128)(2,1)S(1)}, bf16[512,512]{1,0:T(8,128)(2,1)S(1)}) custom-call(bf16[512,1024]{1,0:T(8,128)(2,1)} %tokens.1, f32[8,128]{1,0:T(8,128)S(1)} %pad.4.pos, f32[8,1,1024]{2,1,0:T(1,128)S(1)} %bitcast.3, bf16[512,512]{1,0:T(8,128)(2,1)S(1)} %copy-done, bf16[512,128]{1,0:T(8,128)(2,1)S(1)} %copy-done.2, ...), custom_call_target="tpu_custom_call" | custom-call | tf_op jit(solution)/shard_map/block/pallas_call | solution.py:602
  147.5 1.0 copy.14
  148.4 0.8 copy.15
  (5 shorter events, 0.0 us)
Async XLA Ops:
  0.6 0.7 copy-start.5
  0.6 0.7 copy-start.7
  0.7 0.7 copy-start.8
  1.3 0.7 copy-start.6
  2.0 1.3 copy-start.4
  3.0 1.0 copy-start
  3.0 1.2 copy-start.1
  3.0 1.2 copy-start.2
  3.1 1.2 copy-start.3

commit v5 on v4

--- a/solution.py
+++ b/solution.py
@@ -3,6 +3,7 @@
 
 import jax
 import jax.numpy as jnp
+import numpy as np
 from jax import lax
 from jax.experimental import pallas as pl
 from jax.experimental.pallas import tpu as pltpu
@@ -44,6 +45,10 @@
     return (seq_of(k), tensor_of(k))
 
 
+SHARING = (0, 1, 2, 3, 4, 5, 6, 7, 8, 9, 10, 11, 13, 14, 15, 16, 17)
+ALONE = (0, 1, 2, 4, 6, 8, 9, 13, 14, 15)
+
+
 class Gather:
     def __init__(self, k, slot, half_rows, ring, pair, sibling, ssem, rsem, base=0, along=0, far_by_pair=False):
         self.k, self.slot, self.half = k, slot, half_rows
@@ -51,6 +56,7 @@
         self.ssem, self.rsem, self.base = ssem, rsem, base
         self.along, self.direct = along, 2 * half_rows - 2 * along
         self.far_by_pair = far_by_pair or not sibling
+        self.used = SHARING if sibling else ALONE
         self.sent = []
 
     def at(self, r=0, p=0, c=0):
@@ -68,8 +74,8 @@
         return pltpu.make_async_remote_copy(
             src_ref=ref,
             dst_ref=ref,
-            send_sem=self.ssem.at[self.base + i],
-            recv_sem=self.rsem.at[self.base + i],
+            send_sem=self.ssem.at[self.base + self.used.index(i)],
+            recv_sem=self.rsem.at[self.base + self.used.index(i)],
             device_id=device(self.place(target)),
             device_id_type=MESH,
         )
@@ -192,12 +198,12 @@
 
 
 def block_kernel(
-    tokens, pos, gain, w_query, w_key, w_value, bias, cosine, sine, w_out,
-    mixed, context,
+    tokens, pos, gain_in, w_query, w_key, w_value, b_query, b_key, b_value, freq_in, w_out,
+    mixed, context, gain, bias, freq, cosine, sine,
     x_all, w_all, acc, normed, ssq, inverse, wo_mid, pos_all,
     q, kv_all, wo_all, ctx_all, key_pos, own_pos, top, low, num, mixed_v,
     local_sem, x_ssem, x_rsem, w_ssem, w_rsem, s_ssem, s_rsem, p_ssem, p_rsem, t_ssem, t_rsem,
-    kv_ssem, kv_rsem, wo_ssem, wo_rsem, c_ssem, c_rsem,
+    kv_ssem, kv_rsem, wo_ssem, wo_rsem, c_ssem, c_rsem, out_sem,
 ):
     k = coords()
     me_s, me_t = seq_of(k), tensor_of(k)
@@ -213,6 +219,11 @@
         pltpu.make_async_copy(w_key, w_all.at[me_s, :, pl.ds(qc, kc)], local_sem.at[2]),
         pltpu.make_async_copy(w_value, w_all.at[me_s, :, pl.ds(qc + kc, kc)], local_sem.at[3]),
         pltpu.make_async_copy(pos, pos_all.at[me_s], local_sem.at[4]),
+        pltpu.make_async_copy(gain_in, gain, local_sem.at[6]),
+        pltpu.make_async_copy(b_query, bias.at[:, pl.ds(0, qc)], local_sem.at[7]),
+        pltpu.make_async_copy(b_key, bias.at[:, pl.ds(qc, kc)], local_sem.at[8]),
+        pltpu.make_async_copy(b_value, bias.at[:, pl.ds(qc + kc, kc)], local_sem.at[9]),
+        pltpu.make_async_copy(freq_in, freq, local_sem.at[10]),
     ]
     for c in loads:
         c.start()
@@ -232,7 +243,7 @@
     xg = [
         Gather(
             k, lambda b, h=h: x_all.at[tensor_of(b), pl.ds(h * part_rows, part_rows)], part_rows // 2,
-            "x", "zh", False, x_ssem, x_rsem, base=20 * h, along=ALONG[h],
+            "x", "zh", False, x_ssem, x_rsem, base=10 * h, along=ALONG[h],
         )
         for h in range(2)
     ]
@@ -243,7 +254,7 @@
     kg = [
         Gather(
             k, lambda b, h=h: kv_all.at[kv_rows(h, b)], part_rows // 2, "y", "zl", True,
-            kv_ssem, kv_rsem, base=20 * h, far_by_pair=h == 1,
+            kv_ssem, kv_rsem, base=17 * h, far_by_pair=h == 1,
         )
         for h in range(2)
     ]
@@ -251,7 +262,7 @@
         k, wo_slot, wo_all.shape[0] // 2, "y", "zl", True, wo_ssem, wo_rsem
     )
     cg = [
-        Gather(k, ctx_slot(f, n), n * QT // 2, "x", "zh", False, c_ssem, c_rsem, base=16 * i)
+        Gather(k, ctx_slot(f, n), n * QT // 2, "x", "zh", False, c_ssem, c_rsem, base=8 * i)
         for i, (f, n) in enumerate(CHUNKS)
     ]
 
@@ -337,11 +348,18 @@
         for h in range(2):
             for j in range(part_rows // 128):
                 row = h * (part_rows // 128) + j
-                key_pos[h * 16 + s, :, j * 128 : (j + 1) * 128] = pos_all[s, row : row + 1, :]
+                key_pos[h * 16 + s, :, j * 128 : (j + 1) * 128] = pos_all[s, row : row + 1, :].astype(F32)
         return carry
 
     lax.fori_loop(0, pos_all.shape[0], spread, 0)
-    own_pos[...] = as_columns(pos_all[me_s][0 : rows // 128, :])
+    own_pos[...] = as_columns(pos_all[me_s].astype(F32))
+    lane = lax.broadcasted_iota(jnp.int32, (128, HD), 1)
+    for i in range(rows // 128):
+        r = slice(i * 128, (i + 1) * 128)
+        angles = own_pos[r, :] * freq[...]
+        cosine[r, :] = jnp.cos(angles)
+        turn = jnp.sin(angles)
+        sine[r, :] = jnp.where(lane < HD // 2, -turn, turn)
     def settle():
         for i, (r, p) in enumerate(ORDER[1:]):
             spread_copy(i, moved(k, y=-r, zl=p), moved(k, y=r, zl=p)).wait_recv()
@@ -463,9 +481,9 @@
     event(8, kg[1].s5, sib(1, 2))
     event(9, lambda: close(0), lambda: send_ctx(0))
     event(11, og.s1)
-    event(13, og.s2, cg[0].s1, lambda: close(1), lambda: send_ctx(1))
-    event(14, cg[0].s2, og.s3)
-    event(15, cg[0].s3)
+    event(13, cg[0].s1, lambda: close(1), lambda: send_ctx(1), og.s2)
+    event(14, cg[0].s2)
+    event(15, cg[0].s3, og.s3)
 
     def dispatch(g, first, last):
         if last - first == 1:
@@ -543,17 +561,20 @@
     def output(first, count):
         r = pl.ds(first * QT, count * QT)
 
+        def put_part(c):
+            cols = pl.ds(pl.multiple_of(c * 256, 256), 256)
+            return pltpu.make_async_copy(mixed_v.at[r, cols], mixed.at[r, cols], out_sem.at[0, c])
+
         def part(c, carry):
             cols = pl.ds(pl.multiple_of(c * 256, 256), 256)
             w = wo_all[:, :, :, cols].reshape(ctx_all.shape[1], 256)
             summed = jnp.dot(ctx_all[r, :], w, preferred_element_type=F32)
             mixed_v[r, cols] = (x_all[me_t, r, cols].astype(F32) + summed).astype(BF16)
+            put_part(c).start()
             return carry
 
         lax.fori_loop(0, mixed.shape[1] // 256, part, 0)
-        c = pltpu.make_async_copy(mixed_v.at[r], mixed.at[r], local_sem.at[6 + first])
-        c.start()
-        return c
+        return [put_part(c) for c in range(mixed.shape[1] // 256)]
 
     put = pltpu.make_async_copy(
         ctx_all.at[:, pl.ds(pl.multiple_of(me_t * cw, cw), cw)], context, local_sem.at[5]
@@ -564,9 +585,9 @@
     cg[1].s1()
     cg[1].s2()
     cg[0].s4()
+    og.s4()
     cg[1].s3()
     cg[2].s1()
-    og.s4()
     cg[2].s2()
     cg[0].s5()
     cg[2].s3()
@@ -574,9 +595,8 @@
     og.s5()
     for r, p in ORDER:
         og.recv_sibling(r, p)
-    puts = [put, output(0, 2)]
     ctx_last(2)
-    puts.append(output(2, 2))
+    puts = [put, *output(0, 4)]
     for x in [og, *cg]:
         x.finish()
     for c in puts:
@@ -589,15 +609,9 @@
     wrows = w_query.shape[0]
     heads = qc // HD
     nt, ns = lax.axis_size("tensor"), lax.axis_size("seq")
-    half = HD // 2
-    inv_freq = ROPE_BASE ** (-jnp.arange(half, dtype=F32) * 2.0 / HD)
-    angles = positions.astype(F32)[:, None] * inv_freq[None, :]
-    cos, sin = jnp.cos(angles), jnp.sin(angles)
-    cosine = jnp.concatenate([cos, cos], 1)
-    sine = jnp.concatenate([-sin, sin], 1)
-    bias = jnp.concatenate((b_query, b_key, b_value))[None, :]
-    pos = jnp.pad(positions.astype(F32).reshape(rows // 128, 128), ((0, 8 - rows // 128), (0, 0)))
-    any_, vmem = pl.BlockSpec(memory_space=pltpu.HBM), pl.BlockSpec(memory_space=pltpu.VMEM)
+    inv_freq = ROPE_BASE ** (-np.arange(HD // 2, dtype=np.float64) * 2.0 / HD)
+    freq = jnp.asarray(np.concatenate([inv_freq, inv_freq])[None, :].astype(np.float32))
+    hbm = pl.BlockSpec(memory_space=pltpu.HBM)
     dma = pltpu.SemaphoreType.DMA
     return pl.pallas_call(
         block_kernel,
@@ -606,9 +620,14 @@
             jax.ShapeDtypeStruct((rows, feats), BF16),
             jax.ShapeDtypeStruct((rows, qc), BF16),
         ),
-        in_specs=[any_, any_, vmem, any_, any_, any_, vmem, vmem, vmem, any_],
+        in_specs=[hbm] * 11,
         out_specs=(pl.BlockSpec(memory_space=pl.ANY), pl.BlockSpec(memory_space=pl.ANY)),
         scratch_shapes=[
+            pltpu.VMEM((nt, 1, feats), F32),
+            pltpu.VMEM((1, qc + 2 * kc), F32),
+            pltpu.VMEM((1, HD), F32),
+            pltpu.VMEM((rows, HD), F32),
+            pltpu.VMEM((rows, HD), F32),
             pltpu.VMEM((nt, rows, feats), BF16),
             pltpu.VMEM((ns, wrows, qc + 2 * kc), BF16),
             pltpu.VMEM((rows, qc + 2 * kc), F32),
@@ -616,7 +635,7 @@
             pltpu.VMEM((nt, 8, 128), F32),
             pltpu.VMEM((rows, 128), F32),
             pltpu.VMEM((nt, w_out.shape[0] // 8, w_out.shape[1]), BF16),
-            pltpu.VMEM((ns, 8, 128), F32),
+            pltpu.VMEM((ns, rows // 128, 128), jnp.int32),
             pltpu.VMEM((heads, rows, HD), BF16),
             pltpu.VMEM((ns * rows, 2 * HD), BF16),
             pltpu.VMEM((nt, 8, qc // 8, feats), BF16),
@@ -627,14 +646,17 @@
             pltpu.VMEM((heads, rows, 128), F32),
             pltpu.VMEM((heads, rows, HD), F32),
             pltpu.VMEM((rows, feats), BF16),
-            dma((10,)), dma((40,)), dma((40,)), dma((20,)), dma((20,)),
-            dma((8,)), dma((8,)), dma((16,)), dma((16,)), dma((16,)), dma((16,)),
-            dma((40,)), dma((40,)), dma((20,)), dma((20,)), dma((48,)), dma((48,)),
+            dma((12,)), dma((20,)), dma((20,)), dma((17,)), dma((17,)),
+            dma((7,)), dma((7,)), dma((15,)), dma((15,)), dma((16,)), dma((15,)),
+            dma((34,)), dma((34,)), dma((17,)), dma((17,)), dma((24,)), dma((24,)), dma((1, 4)),
         ],
         compiler_params=pltpu.CompilerParams(
-            collective_id=0, has_side_effects=True, vmem_limit_bytes=50 * 1024 * 1024
+            collective_id=0, has_side_effects=True, vmem_limit_bytes=58 * 1024 * 1024
         ),
-    )(tokens, pos, norm_gain.reshape(nt, 1, feats), w_query, w_key, w_value, bias, cosine, sine, w_out)
+    )(
+        tokens, positions.reshape(rows // 128, 128), norm_gain.reshape(nt, 1, feats), w_query, w_key, w_value,
+        b_query[None, :], b_key[None, :], b_value[None, :], freq, w_out,
+    )
 
 
 def solution(mesh):

time: 152 us -> 149 us (0.980); the launches traced: 149 us -> 149 us
  Pallas kernels: 143 us -> 145 us
    pallas_call x1, Pallas kernels: 143 us -> 145 us  [shards(): pl.pallas_call(block_kernel, name='block', out_shape=(jax.ShapeDtypeStruc...]
    unnamed x20 -> x4, local copies, waits for them, and re-layouts: 4.1 us -> 3.12 us
where the time goes in v5:
time: 149 us
  Pallas kernels  145 us (97%)
  local copies, waits for them, and re-layouts  3.12 us (2%)
    pallas_call x1, Pallas kernels, shards(): pl.pallas_call(block_kernel, name='block', out_shape=(jax.ShapeDtypeStruc...  145 us
    unnamed x4, local copies, waits for them, and re-layouts  3.12 us

profile of v5, /device:TPU:0, one launch (start us, length us, event | category | flops | bytes accessed | tf_op | source)
XLA Modules:
  0.0 149.0 jit_solution(2708678794404795857)
XLA Ops:
  0.6 145.2 %block.1 = (bf16[512,1024]{1,0:T(8,128)(2,1)}, bf16[512,512]{1,0:T(8,128)(2,1)}) custom-call(bf16[512,1024]{1,0:T(8,128)(2,1)} %tokens.1, s32[4,128]{1,0:T(4,128)} %bitcast.6, f32[8,1,1024]{2,1,0:T(1,128)} %bitcast.5, bf16[512,512]{1,0:T(8,128)(2,1)} %w_query.1, bf16[512,128]{1,0:T(8,128)(2,1)} %w_key.1, bf16[512,128]{1,0:T(8,128)(2,1)} %w_value.1, ...), custom_call_target="tpu_custom_call" | custom-call | tf_op jit(solution)/shard_map/block/pallas_call | solution.py:616
  145.9 0.0 copy-start
  145.9 2.3 %copy.15 = bf16[512,1024]{1,0:T(8,128)(2,1)} copy(bf16[512,1024]{1,0:T(8,128)(2,1)} %get-tuple-element.4) | data formatting | bytes 2097152
  148.2 0.0 copy-done
  148.2 0.8 copy.16
Async XLA Ops:
  145.9 2.3 %copy-start = (bf16[512,512]{1,0:T(8,128)(2,1)S(1)}, bf16[512,512]{1,0:T(8,128)(2,1)}, u32[]{:S(2)}) copy-start(bf16[512,512]{1,0:T(8,128)(2,1)} %get-tuple-element.5) | copy-start | bytes 1572868

commit v6 on v5

--- a/solution.py
+++ b/solution.py
@@ -45,7 +45,7 @@
     return (seq_of(k), tensor_of(k))
 
 
-SHARING = (0, 1, 2, 3, 4, 5, 6, 7, 8, 9, 10, 11, 13, 14, 15, 16, 17)
+SHARING = (0, 1, 2, 3, 4, 5, 6, 7, 8, 9, 10, 11, 13, 14, 15, 16, 17, 18)
 ALONE = (0, 1, 2, 4, 6, 8, 9, 13, 14, 15)
 
 
@@ -87,9 +87,9 @@
     def recv(self, i, block, half=None):
         self.copy(i, block, (0, 0, 1) if self.sibling else (1, 0, 0), half).wait_recv()
 
-    def share(self, i, block):
+    def share(self, i, block, half=None):
         if self.sibling:
-            self.send(i, block, self.at(c=1))
+            self.send(i, block, self.at(c=1), half)
 
     def s0(self):
         self.s0_ring()
@@ -144,15 +144,21 @@
             if self.along:
                 self.recv(14, self.at(2, 1), (self.direct, self.along))
                 self.recv(15, self.at(2, 1), (self.direct + self.along, self.along))
+            self.share(17, self.at(2, 1))
         else:
             self.recv(13, self.at(2, 1), 0)
+            self.share(17, self.at(2, 1), 0)
             self.recv(15, self.at(2, 1), 1)
-        self.share(17, self.at(2, 1))
+            self.share(18, self.at(2, 1), 1)
 
     SHARED = {(0, 0): 3, (-1, 0): 5, (1, 0): 7, (0, 1): 10, (2, 0): 11, (-1, 1): 14, (1, 1): 16, (2, 1): 17}
 
     def recv_sibling(self, r, p):
-        self.recv(self.SHARED[(r, p)], self.at(r, p, 1))
+        if (r, p) == (2, 1) and not self.far_by_pair:
+            self.recv(17, self.at(r, p, 1), 0)
+            self.recv(18, self.at(r, p, 1), 1)
+        else:
+            self.recv(self.SHARED[(r, p)], self.at(r, p, 1))
 
     def finish(self):
         for i, block, target, half in self.sent:
@@ -192,7 +198,7 @@
 
 
 QT = 128
-CHUNKS = ((0, 2), (2, 1), (3, 1))
+CHUNKS = ((0, 1), (1, 1), (2, 1), (3, 1))
 GROUP = 2
 ALONG = (64, 0)
 
@@ -254,7 +260,7 @@
     kg = [
         Gather(
             k, lambda b, h=h: kv_all.at[kv_rows(h, b)], part_rows // 2, "y", "zl", True,
-            kv_ssem, kv_rsem, base=17 * h, far_by_pair=h == 1,
+            kv_ssem, kv_rsem, base=18 * h, far_by_pair=h == 1,
         )
         for h in range(2)
     ]
@@ -473,17 +479,17 @@
 
     event(0, sib(0, 0))
     event(2, kg[0].s3, kg[0].s4, sib(0, -1))
-    event(3, kg[1].s1, kg[1].s2, sib(0, 1))
-    event(4, settled, og.s0_ring, sib(1, 0), kg[0].s5)
-    event(5, kg[1].s3, og.s0_pair, sib(0, 2))
+    event(3, kg[1].s1, kg[1].s2, settled, og.s0_ring, sib(0, 1))
+    event(4, kg[1].s3, og.s0_pair, sib(1, 0), kg[0].s5)
+    event(5, sib(0, 2))
     event(6, kg[1].s4, sib(1, -1))
     event(7, sib(1, 1), settle_sends)
     event(8, kg[1].s5, sib(1, 2))
-    event(9, lambda: close(0), lambda: send_ctx(0))
-    event(11, og.s1)
-    event(13, cg[0].s1, lambda: close(1), lambda: send_ctx(1), og.s2)
-    event(14, cg[0].s2)
-    event(15, cg[0].s3, og.s3)
+    event(9, lambda: close(0), lambda: send_ctx(0), lambda: close(1), lambda: send_ctx(1))
+    event(10, og.s1)
+    event(12, cg[0].s1, og.s2, cg[0].s2)
+    event(13, lambda: close(2), lambda: send_ctx(2), cg[1].s1)
+    event(14, cg[0].s3)
 
     def dispatch(g, first, last):
         if last - first == 1:
@@ -556,8 +562,10 @@
 
     lax.fori_loop(0, 4 * tiles, step, 0)
 
-    close(2)
-    send_ctx(2)
+    close(3)
+    send_ctx(3)
+    cg[2].s1()
+    cg[1].s2()
     def output(first, count):
         r = pl.ds(first * QT, count * QT)
 
@@ -582,20 +590,22 @@
     put.start()
     kg[0].finish()
     kg[1].finish()
-    cg[1].s1()
-    cg[1].s2()
+    cg[1].s3()
+    og.s3()
     cg[0].s4()
+    cg[3].s1()
     og.s4()
-    cg[1].s3()
-    cg[2].s1()
     cg[2].s2()
+    cg[3].s2()
+    cg[2].s3()
+    cg[3].s3()
     cg[0].s5()
-    cg[2].s3()
     ctx_last(1)
     og.s5()
     for r, p in ORDER:
         og.recv_sibling(r, p)
     ctx_last(2)
+    ctx_last(3)
     puts = [put, *output(0, 4)]
     for x in [og, *cg]:
         x.finish()
@@ -646,9 +656,9 @@
             pltpu.VMEM((heads, rows, 128), F32),
             pltpu.VMEM((heads, rows, HD), F32),
             pltpu.VMEM((rows, feats), BF16),
-            dma((12,)), dma((20,)), dma((20,)), dma((17,)), dma((17,)),
+            dma((12,)), dma((20,)), dma((20,)), dma((18,)), dma((18,)),
             dma((7,)), dma((7,)), dma((15,)), dma((15,)), dma((16,)), dma((15,)),
-            dma((34,)), dma((34,)), dma((17,)), dma((17,)), dma((24,)), dma((24,)), dma((1, 4)),
+            dma((36,)), dma((36,)), dma((18,)), dma((18,)), dma((32,)), dma((32,)), dma((1, 4)),
         ],
         compiler_params=pltpu.CompilerParams(
             collective_id=0, has_side_effects=True, vmem_limit_bytes=58 * 1024 * 1024

time: 149 us -> 146 us (0.980)
  Pallas kernels: 145 us -> 142 us
    pallas_call x1, Pallas kernels: 145 us -> 142 us  [shards(): pl.pallas_call(block_kernel, name='block', out_shape=(jax.ShapeDtypeStruc...]
where the time goes in v6:
time: 146 us; the launch traced here: 145 us
  Pallas kernels  142 us (97%)
  local copies, waits for them, and re-layouts  3.12 us (2%)
    pallas_call x1, Pallas kernels, shards(): pl.pallas_call(block_kernel, name='block', out_shape=(jax.ShapeDtypeStruc...  142 us
    unnamed x4, local copies, waits for them, and re-layouts  3.12 us

profile of v6, /device:TPU:0, one launch (start us, length us, event | category | flops | bytes accessed | tf_op | source)
XLA Modules:
  0.0 145.4 jit_solution(250305839403062657)
XLA Ops:
  0.6 141.6 %block.1 = (bf16[512,1024]{1,0:T(8,128)(2,1)}, bf16[512,512]{1,0:T(8,128)(2,1)}) custom-call(bf16[512,1024]{1,0:T(8,128)(2,1)} %tokens.1, s32[4,128]{1,0:T(4,128)} %bitcast.6, f32[8,1,1024]{2,1,0:T(1,128)} %bitcast.5, bf16[512,512]{1,0:T(8,128)(2,1)} %w_query.1, bf16[512,128]{1,0:T(8,128)(2,1)} %w_key.1, bf16[512,128]{1,0:T(8,128)(2,1)} %w_value.1, ...), custom_call_target="tpu_custom_call" | custom-call | tf_op jit(solution)/shard_map/block/pallas_call | solution.py:626
  142.3 0.0 copy-start
  142.3 2.3 %copy.15 = bf16[512,1024]{1,0:T(8,128)(2,1)} copy(bf16[512,1024]{1,0:T(8,128)(2,1)} %get-tuple-element.4) | data formatting | bytes 2097152
  144.6 0.0 copy-done
  144.6 0.8 copy.16
Async XLA Ops:
  142.3 2.3 %copy-start = (bf16[512,512]{1,0:T(8,128)(2,1)S(1)}, bf16[512,512]{1,0:T(8,128)(2,1)}, u32[]{:S(2)}) copy-start(bf16[512,512]{1,0:T(8,128)(2,1)} %get-tuple-element.5) | copy-start | bytes 1572868

commit v7 on v6

--- a/solution.py
+++ b/solution.py
@@ -380,7 +380,7 @@
         settle_own.wait()
 
     wg.s5()
-    for r, p in ORDER:
+    for r, p in ORDER[:-1]:
         wg.recv_sibling(r, p)
 
     cos_sin = (cosine, sine)
@@ -389,6 +389,12 @@
         first = h * part_rows
 
         def block(step, carry):
+            if h == 0:
+
+                @pl.when(step == 7)
+                def _():
+                    wg.recv_sibling(2, 1)
+
             if h == 1:
 
                 @pl.when(step == 5)
@@ -404,7 +410,10 @@
 
             dx = pick(step, [r % 4 for r, _ in ORDER])
             dz = pick(step, [p for _, p in ORDER])
-            t = ((k["zh"] + dz) % 2) * 4 + (k["x"] + dx) % 4
+            if h == 0:
+                t = ((k["y"] + dx) % 4) * 2 + (k["zl"] + dz) % 2
+            else:
+                t = ((k["zh"] + dz) % 2) * 4 + (k["x"] + dx) % 4
             g = gain[t]
             for i in range(part_rows // 128):
                 r = pl.ds(first + i * 128, 128)

time: 146 us -> 147 us (level)
  no operation moved by 1% of the time
where the time goes in v7:
time: 147 us; the launch traced here: 146 us
  Pallas kernels  143 us (97%)
  local copies, waits for them, and re-layouts  3.12 us (2%)
    pallas_call x1, Pallas kernels, shards(): pl.pallas_call(block_kernel, name='block', out_shape=(jax.ShapeDtypeStruc...  143 us
    unnamed x4, local copies, waits for them, and re-layouts  3.12 us

profile of v7, /device:TPU:0, one launch (start us, length us, event | category | flops | bytes accessed | tf_op | source)
XLA Modules:
  0.0 146.5 jit_solution(3938591833210922984)
XLA Ops:
  0.6 142.7 %block.1 = (bf16[512,1024]{1,0:T(8,128)(2,1)}, bf16[512,512]{1,0:T(8,128)(2,1)}) custom-call(bf16[512,1024]{1,0:T(8,128)(2,1)} %tokens.1, s32[4,128]{1,0:T(4,128)} %bitcast.6, f32[8,1,1024]{2,1,0:T(1,128)} %bitcast.5, bf16[512,512]{1,0:T(8,128)(2,1)} %w_query.1, bf16[512,128]{1,0:T(8,128)(2,1)} %w_key.1, bf16[512,128]{1,0:T(8,128)(2,1)} %w_value.1, ...), custom_call_target="tpu_custom_call" | custom-call | tf_op jit(solution)/shard_map/block/pallas_call | solution.py:635
  143.3 0.0 copy-start
  143.3 2.3 %copy.15 = bf16[512,1024]{1,0:T(8,128)(2,1)} copy(bf16[512,1024]{1,0:T(8,128)(2,1)} %get-tuple-element.4) | data formatting | bytes 2097152
  145.7 0.0 copy-done
  145.7 0.8 copy.16
Async XLA Ops:
  143.3 2.3 %copy-start = (bf16[512,512]{1,0:T(8,128)(2,1)S(1)}, bf16[512,512]{1,0:T(8,128)(2,1)}, u32[]{:S(2)}) copy-start(bf16[512,512]{1,0:T(8,128)(2,1)} %get-tuple-element.5) | copy-start | bytes 1572868
